TPU v7x, 128 devices: a whole 4x4x4 slice. The times are simulated.
128 devices in a mesh: ga: 16 (over x, y), band: 8 (over z, core).
Axes of the slice: x: 4, y: 4, z: 4, core: 2. Of those that a mesh axis runs over, the one named last changes fastest.
Arguments:
- psi: bfloat16 [2, 16, 96, 2048], P(None, 'band', None, 'ga'), may hold values from -6 to 6
- vloc: float32 [96, 9216], P('ga'), may hold values from 0.5 to 1.5
- dv: float32 [96, 9216], P('ga'), may hold values from -6 to 6
- beta: float32 [2, 128, 96, 2048], P(None, None, None, 'ga'), may hold values from -0.02734375 to 0.02734375
- dij: float32 [2, 4, 4], replicated, may hold values from -1 to 1.5, as said below
- atom_type: int32 [32], replicated, may hold values from 0 to 1
- stick_xy: int32 [2048], replicated, may hold values from 0 to 9215, as said below
- band_shift: float32 [16], P('band'), may hold values from 0.3 to 3
Outputs:
- response: float32 [2, 16, 96, 2048], P(None, 'band', None, 'ga')
- density: float32 [96, 9216], P('ga', 'band')
Inputs may be any that keep to these rules, and one draw needn't show every extreme that they name: `stick_xy`: 2048 distinct columns, each with both frequencies f(y) and f(x) in -(32) to 31. `dij`: each of the 2 matrices is symmetric positive definite with diagonal at least 0.5.
All inputs are finite; a program needn't handle non-finite values.
Results may differ from a plain program's by a relative error of at most 0.0003.
Values may be sent and summed in bfloat16 or wider, within the bound.
A program may use at most 128 MiB of HBM per device.

v0:
```python
import functools
import math

import jax
import jax.numpy as jnp
import numpy as np
from jax import lax
from jax.experimental import pallas as pl
from jax.experimental.pallas import tpu as pltpu
from jax.sharding import PartitionSpec as P

GRID = 96
SIDE = 64
GROUPS = 16
PLANES = 6
ROWS = 24
MESH = pl.DeviceIdType.MESH
f32 = jnp.float32
bf16 = jnp.bfloat16


def complex_table(angle):
    cos, sin = np.cos(angle), np.sin(angle)
    return np.array([[cos, -sin], [sin, cos]]) / math.sqrt(GRID)


def halves(table):
    high = np.asarray(table, np.float32).astype(jnp.bfloat16)
    low = (table - high.astype(np.float64)).astype(jnp.bfloat16)
    return high, low


def tables(bands):
    unit = 2.0 * math.pi / GRID
    cells = np.arange(GRID)
    freqs = np.arange(SIDE) - SIDE // 2
    along_z = complex_table(unit * (cells[:, None] * cells[None, :] % GRID))
    along_z = along_z.reshape(2, 2, GROUPS, PLANES, GRID)
    z_table = np.einsum("oidpk,be->dopbiek", along_z, np.eye(bands))
    z_table = z_table.reshape(GROUPS * 2 * PLANES * bands, 2 * bands * GRID)
    along_x = np.zeros((2, 2, SIDE, 128))
    along_x[..., :GRID] = complex_table(unit * (freqs[:, None] * cells[None, :] % GRID))
    x_table = np.einsum("oikx,be->ibkoex", along_x, np.eye(2)).reshape(256, 512)
    along_y = complex_table(unit * (cells[:, None] * freqs[None, :] % GRID))
    along_y = along_y.reshape(2, 2, GRID, 16, 4)
    y_table = np.einsum("oiygl->oyilg", along_y).reshape(192, 128)
    out = []
    for table in (z_table, z_table.T, x_table, x_table.T, y_table):
        out.extend(halves(np.ascontiguousarray(table)))
    high, low = halves(np.ascontiguousarray(y_table.T))
    out.append(np.concatenate([high, high, low], axis=1))
    return [jnp.asarray(t) for t in out]


def dot(a, b):
    return lax.dot_general(a, b, (((1,), (0,)), ((), ())), preferred_element_type=f32)


def dot_nt(a, b):
    return lax.dot_general(a, b, (((1,), (1,)), ((), ())), preferred_element_type=f32)


def split(x):
    high = x.astype(bf16)
    return high, (x - high.astype(f32)).astype(bf16)


def left(high, low, x):
    xh, xl = split(x)
    return dot(
        jnp.concatenate([high, high, low], axis=1), jnp.concatenate([xh, xl, xh], axis=0)
    )


def right(ah, al, high, low):
    return dot(
        jnp.concatenate([ah, al, ah], axis=1), jnp.concatenate([high, high, low], axis=0)
    )


def row_sum(x):
    return jnp.sum(jnp.sum(x.reshape(-1, 8, 128), axis=0), axis=0, keepdims=True)


def lane_total(row):
    return jnp.sum(row, axis=1, keepdims=True)


def kernel(
    shift, dij, psi, vloc, dv, beta_hbm, kind, sticks,
    zh, zl, zth, ztl, xh, xl, xth, xtl, yh, yl, yt3,
    response, density,
    beta, occupied, onehot, mask, send, recv, small_send, small_recv,
    part_send, part_recv, lhs, grid, eh, el, dh, dl, psi_field, field0, field1,
    q, proj, coef, couple, vec, image, kin, own, dens,
    beta_sem, psi_ssem, psi_rsem, ssem, rsem, tssem, trsem, dssem, drsem,
):
    me = lax.axis_index("ga")
    mb = lax.axis_index("band")
    nb = 8

    barrier = pltpu.get_barrier_semaphore()

    def greet_ga(k, c):
        pl.semaphore_signal(
            barrier, inc=1, device_id=(lax.rem(me + k, GROUPS), mb), device_id_type=MESH
        )
        return c

    def greet_band(k, c):
        pl.semaphore_signal(
            barrier, inc=1, device_id=(me, lax.rem(mb + k, nb)), device_id_type=MESH
        )
        return c

    lax.fori_loop(1, GROUPS, greet_ga, 0)
    lax.fori_loop(1, nb, greet_band, 0)
    beta_copy = pltpu.make_async_copy(beta_hbm, beta, beta_sem)
    beta_copy.start()

    def ga_copy(rnd, k):
        other = lax.rem(me + k, GROUPS)
        return pltpu.make_async_remote_copy(
            src_ref=send.at[rnd, other],
            dst_ref=recv.at[rnd, me],
            send_sem=ssem.at[rnd, other],
            recv_sem=rsem.at[rnd, me],
            device_id=(other, mb),
            device_id_type=MESH,
        )

    def ga_landed(rnd, k):
        other = lax.rem(me + k, GROUPS)
        return pltpu.make_async_remote_copy(
            src_ref=send.at[rnd, other],
            dst_ref=recv.at[rnd, other],
            send_sem=ssem.at[rnd, other],
            recv_sem=rsem.at[rnd, other],
            device_id=(other, mb),
            device_id_type=MESH,
        )

    def exchange(rnd):
        def body(k, c):
            ga_copy(rnd, k).start()
            return c

        lax.fori_loop(1, GROUPS, body, 0)
        recv[rnd, me] = send[rnd, me]

    def arrived(rnd):
        def body(k, c):
            ga_landed(rnd, k).wait_recv()
            return c

        lax.fori_loop(1, GROUPS, body, 0)

    def small_copy(rnd, k, slot):
        other = lax.rem(me + k, GROUPS)
        return pltpu.make_async_remote_copy(
            src_ref=small_send.at[rnd],
            dst_ref=small_recv.at[rnd, me if slot is None else other],
            send_sem=tssem.at[rnd, other],
            recv_sem=trsem.at[rnd, me if slot is None else other],
            device_id=(other, mb),
            device_id_type=MESH,
        )

    def small_exchange(rnd):
        def body(k, c):
            small_copy(rnd, k, None).start()
            return c

        lax.fori_loop(1, GROUPS, body, 0)
        small_recv[rnd, me] = small_send[rnd]

    def small_total(rnd):
        def body(k, c):
            small_copy(rnd, k, 0).wait_recv()
            return c

        lax.fori_loop(1, GROUPS, body, 0)
        return jnp.sum(small_recv[rnd], axis=0)

    def psi_copy(k, slot):
        other = lax.rem(mb + k, nb)
        return pltpu.make_async_remote_copy(
            src_ref=psi,
            dst_ref=occupied.at[mb if slot is None else other],
            send_sem=psi_ssem.at[other],
            recv_sem=psi_rsem.at[mb if slot is None else other],
            device_id=(me, other),
            device_id_type=MESH,
        )

    def part_copy(k, slot):
        other = lax.rem(mb + k, nb)
        return pltpu.make_async_remote_copy(
            src_ref=part_send.at[other],
            dst_ref=part_recv.at[mb if slot is None else other],
            send_sem=dssem.at[other],
            recv_sem=drsem.at[mb if slot is None else other],
            device_id=(me, other),
            device_id_type=MESH,
        )

    wide = psi[...].reshape(384, 128)
    send[0] = dot(
        jnp.concatenate([zh[...], zl[...]], axis=1), jnp.concatenate([wide, wide], axis=0)
    ).reshape(GROUPS, ROWS, 128)
    pl.semaphore_wait(barrier, GROUPS - 1 + nb - 1)
    exchange(0)

    def psi_out(k, c):
        psi_copy(k, None).start()
        return c

    lax.fori_loop(1, nb, psi_out, 0)
    occupied[mb] = psi[...]

    def places(xy):
        flat = xy.astype(f32)
        y = jnp.floor((flat + 0.5) * (1.0 / GRID))
        x = flat - GRID * y
        fy = jnp.where(y >= GRID // 2, y - GRID, y)
        fx = jnp.where(x >= GRID // 2, x - GRID, x)
        return fy, fx

    fy, fx = places(sticks[...])
    ky = fy + SIDE // 2
    kx = fx + SIDE // 2
    high = jnp.floor(ky * 0.25)
    low = (ky - 4.0 * high) * SIDE + kx
    own[0:1, :] = low
    own[1:2, :] = high
    mask[...] = (
        lax.broadcasted_iota(jnp.int32, (16, 2048), 0).astype(f32) == own[1:2, :]
    ).astype(f32)

    def fill(k, c):
        lanes = pl.ds(pl.multiple_of(k * 256, 256), 256)
        ids = lax.broadcasted_iota(jnp.int32, (256, 256), 0).astype(f32)
        onehot[:, lanes] = (ids == own[0:1, lanes]).astype(f32).astype(bf16)
        return c

    lax.fori_loop(0, 8, fill, 0)
    mine = sticks[:, pl.ds(pl.multiple_of(me * 128, 128), 128)]
    oy, ox = places(mine)
    kz = lax.broadcasted_iota(jnp.int32, (GRID, 128), 0).astype(f32)
    fz = jnp.where(kz >= GRID // 2, kz - GRID, kz)
    kin[...] = (fz * fz + (oy * oy + ox * ox)) * (4.0 / (GRID * GRID))

    row = lax.broadcasted_iota(jnp.int32, (128, 128), 0)
    lane = lax.broadcasted_iota(jnp.int32, (128, 128), 1)
    same = (row // 4) == (lane // 4)
    first = kind[...] == 0
    total = jnp.zeros((128, 128), f32)
    for i in range(4):
        for k in range(4):
            value = jnp.where(first, dij[i * 4 + k], dij[16 + i * 4 + k])
            here = same & ((row % 4) == i) & ((lane % 4) == k)
            total = total + jnp.where(here, value, 0.0)
    couple[...] = total
    ones = jnp.ones((256, 128), bf16)

    def fill_planes(rnd, out):

        def body(src, c):
            piece = recv[rnd, src]
            upper = piece.astype(bf16).astype(f32)
            lower = piece - upper
            cols = pl.ds(pl.multiple_of(src * 128, 128), 128)
            keep = mask[:, cols]
            for r in range(ROWS):
                lhs[16 * r : 16 * r + 16, cols] = (
                    jnp.broadcast_to(upper[r : r + 1], (16, 128)) * keep
                ).astype(bf16)
                lhs[384 + 16 * r : 400 + 16 * r, cols] = (
                    jnp.broadcast_to(lower[r : r + 1], (16, 128)) * keep
                ).astype(bf16)
            return c

        lax.fori_loop(0, GROUPS, body, 0)
        both = dot_nt(lhs[...], onehot[...])
        grid[...] = both[0:384] + both[384:768]
        for t in range(2):
            lanes = slice(128 * t, 128 * t + 128)
            data = jnp.concatenate([grid[0:192, lanes], grid[192:384, lanes]], axis=1)
            ah, al = split(data)
            along = right(ah, al, xh[...], xl[...])
            uh, ul = split(along)
            eh[...] = uh
            el[...] = ul
            for c in range(2):
                for j in range(2):
                    rows = slice(16 * (4 * c + 2 * t + j), 16 * (4 * c + 2 * t + j) + 16)
                    cols = slice(128 * (2 * c + j), 128 * (2 * c + j) + 128)
                    for i in range(12):
                        dh[rows, 128 * i : 128 * i + 128] = eh[16 * i : 16 * i + 16, cols]
                        dl[rows, 128 * i : 128 * i + 128] = el[16 * i : 16 * i + 16, cols]
        for part in range(6):
            lanes = slice(256 * part, 256 * part + 256)
            out[:, lanes] = dot(
                jnp.concatenate([yh[...], yh[...], yl[...]], axis=1),
                jnp.concatenate([dh[:, lanes], dl[:, lanes], dh[:, lanes]], axis=0),
            )

    def to_sticks(rnd, potential, source):
        for p in range(PLANES):
            lanes = slice(256 * p, 256 * p + 256)
            pot = potential[:, 128 * p : 128 * p + 128]
            pot = jnp.concatenate([pot, pot], axis=1)
            pot = jnp.concatenate([pot, pot], axis=0)
            ah, al = split(source[:, lanes] * pot)
            along = dot(yt3[...], jnp.concatenate([ah, al, ah], axis=0))
            uh, ul = split(along)
            dh[:, lanes] = uh
            dl[:, lanes] = ul
        for t in range(2):
            for c in range(2):
                for j in range(2):
                    rows = slice(16 * (4 * c + 2 * t + j), 16 * (4 * c + 2 * t + j) + 16)
                    cols = slice(128 * (2 * c + j), 128 * (2 * c + j) + 128)
                    for i in range(12):
                        eh[16 * i : 16 * i + 16, cols] = dh[rows, 128 * i : 128 * i + 128]
                        el[16 * i : 16 * i + 16, cols] = dl[rows, 128 * i : 128 * i + 128]
            along = right(eh[...], el[...], xth[...], xtl[...])
            uh, ul = split(along)
            lanes = slice(128 * t, 128 * t + 128)
            for c in range(2):
                q[192 * c : 192 * c + 192, lanes] = uh[:, 128 * c : 128 * c + 128]
                q[384 + 192 * c : 576 + 192 * c, lanes] = ul[:, 128 * c : 128 * c + 128]

        def body(k, carry):
            lanes = pl.ds(pl.multiple_of(k * 256, 256), 256)
            place = onehot[:, lanes]
            keep = mask[:, lanes]
            both = dot(q[...], place)
            found = both[0:384] + both[384:768]
            picked = jnp.sum(found.reshape(ROWS, 16, 256) * keep[None], axis=1)
            send[rnd, 2 * k] = picked[:, 0:128]
            send[rnd, 2 * k + 1] = picked[:, 128:256]
            return carry

        lax.fori_loop(0, 8, body, 0)

    def z_forward(rnd):
        return left(zth[...], ztl[...], recv[rnd].reshape(384, 128))

    def project(load, count, source):
        def body(j, c):
            p0, p1 = load(j)
            for b in range(2):
                v0 = source[96 * b : 96 * b + 96, :]
                v1 = source[192 + 96 * b : 288 + 96 * b, :]
                proj[b, pl.ds(j, 1), :] = row_sum(p0 * v0 + p1 * v1)
                proj[2 + b, pl.ds(j, 1), :] = row_sum(p0 * v1 - p1 * v0)
            return c

        lax.fori_loop(0, count, body, 0)

    def projections(o, count):
        ph, pl_ = split(proj[o, 0:count, :])
        one = jnp.ones((8, 128), bf16)
        return dot_nt(
            jnp.concatenate([one, one], axis=1), jnp.concatenate([ph, pl_], axis=1)
        )[0:1, :]

    def spread(matrix, values):
        count = matrix.shape[0]
        for o in range(4):
            mh, ml = split(matrix * values[o : o + 1, :])
            coef[o, 0:count, :] = dot(jnp.concatenate([mh, ml], axis=1), ones)

    def apply(load, count, base):
        rows = 24
        for z in range(GRID // rows):

            def body(j, acc):
                p0, p1 = load(j, z * rows, rows)
                out = []
                for b in range(2):
                    cr = coef[b, pl.ds(j, 1), :]
                    ci = coef[2 + b, pl.ds(j, 1), :]
                    out.append(acc[2 * b] + (p0 * cr - p1 * ci))
                    out.append(acc[2 * b + 1] + (p0 * ci + p1 * cr))
                return tuple(out)

            init = tuple(
                base[192 * c + 96 * b + z * rows : 192 * c + 96 * b + z * rows + rows, :]
                for b in range(2)
                for c in range(2)
            )
            done = lax.fori_loop(0, count, body, init)
            for b in range(2):
                for c in range(2):
                    at = 192 * c + 96 * b + z * rows
                    image[at : at + rows, :] = done[2 * b + c]

    def beta_rows(j, at=0, rows=GRID):
        return beta[0, j, at : at + rows, :], beta[1, j, at : at + rows, :]

    def psi_rows(m, at=0, rows=GRID):
        owner, b = m // 2, m % 2
        return (
            occupied[owner, 0, b, at : at + rows, :].astype(f32),
            occupied[owner, 1, b, at : at + rows, :].astype(f32),
        )

    arrived(0)
    fill_planes(0, psi_field)
    to_sticks(1, dv, psi_field)
    exchange(1)

    def psi_in(k, c):
        psi_copy(k, 0).wait_recv()
        return c

    arrived(1)
    vec[1] = z_forward(1)
    lax.fori_loop(1, nb, psi_in, 0)

    project(psi_rows, 16, vec.at[1])
    small_send[0] = jnp.zeros((16, 128), f32)
    for o in range(4):
        small_send[0, o : o + 1, 0:16] = projections(o, 16)
    small_exchange(0)
    found = small_total(0) * (1.0 / (2.0 * GRID * 2048))
    eye = (row[0:16] == lane[0:16]).astype(f32)
    spread(eye, found)
    vec[1] = -vec[1]
    apply(psi_rows, 16, vec.at[1])
    vec[0] = image[...]

    def transform_out(rnd, source):
        send[rnd] = left(zh[...], zl[...], source[...]).reshape(GROUPS, ROWS, 128)
        exchange(rnd)

    def stick_sum(a, b, weight=None):
        out = []
        for n in range(2):
            s0 = slice(96 * n, 96 * n + 96)
            s1 = slice(192 + 96 * n, 288 + 96 * n)
            both = a[s0, :] * b[s0, :] + a[s1, :] * b[s1, :]
            if weight is not None:
                both = both * (kin[...] + shift[n])
            out.append(row_sum(both))
        return out

    def grid_sum(a, b):
        out = []
        for n in range(2):
            total = jnp.zeros((1, 128), f32)
            for p in range(PLANES):
                lanes = slice(128 * (2 * p + n), 128 * (2 * p + n) + 128)
                pot = vloc[:, 128 * p : 128 * p + 128]
                both = a[0:96, lanes] * b[0:96, lanes] + a[96:192, lanes] * b[96:192, lanes]
                total = total + row_sum(both * pot)
            out.append(total)
        return out

    def band_dots(values, coupled):
        both = values * coupled
        return [lane_total(both[b : b + 1] + both[2 + b : 3 + b]) for b in range(2)]

    ch, cl = split(couple[...])

    def coupled_rows(values):
        vh, vl = split(values)
        return dot_nt(
            jnp.concatenate([vh, vl, vh], axis=1), jnp.concatenate([ch, ch, cl], axis=1)
        )

    direction = vec.at[0]
    transform_out(2, direction)
    beta_copy.wait()
    project(beta_rows, 128, direction)
    small_send[1] = jnp.zeros((16, 128), f32)
    for o in range(4):
        small_send[1, o : o + 1, :] = projections(o, 128)
    norms = stick_sum(direction, direction)
    curves = stick_sum(direction, direction, True)
    arrived(2)
    fill_planes(2, field0)
    local = grid_sum(field0, field0)
    for b in range(2):
        small_send[1, 4 + b : 5 + b, :] = norms[b]
        small_send[1, 6 + b : 7 + b, :] = curves[b] + local[b]
    small_exchange(1)
    to_sticks(3, vloc, field0)
    exchange(3)
    sums = small_total(1)
    values0 = sums[0:4]
    coupled0 = coupled_rows(sums[0:8])[0:4]
    nonlocal0 = band_dots(values0, coupled0)
    norm0 = [lane_total(sums[4 + b : 5 + b]) for b in range(2)]
    curve0 = [lane_total(sums[6 + b : 7 + b]) + nonlocal0[b] for b in range(2)]
    alpha0 = [norm0[b] / curve0[b] for b in range(2)]
    spread(couple[...], values0)
    for c in range(2):
        for b in range(2):
            at = slice(192 * c + 96 * b, 192 * c + 96 * b + 96)
            vec[1, at, :] = direction[at, :] * (kin[...] + shift[b])
    apply(beta_rows, 128, vec.at[1])
    arrived(3)
    image[...] += z_forward(3)
    residual = vec.at[1]
    for c in range(2):
        for b in range(2):
            at = slice(192 * c + 96 * b, 192 * c + 96 * b + 96)
            residual[at, :] = direction[at, :] - alpha0[b] * image[at, :]

    transform_out(4, residual)
    project(beta_rows, 128, residual)
    small_send[2] = jnp.zeros((16, 128), f32)
    for o in range(4):
        small_send[2, o : o + 1, :] = projections(o, 128)
    norms = stick_sum(residual, residual)
    selfs = stick_sum(residual, residual, True)
    crosses = stick_sum(residual, direction, True)
    arrived(4)
    fill_planes(4, field1)
    self_local = grid_sum(field1, field1)
    cross_local = grid_sum(field1, field0)
    for b in range(2):
        small_send[2, 4 + b : 5 + b, :] = norms[b]
        small_send[2, 6 + b : 7 + b, :] = selfs[b] + self_local[b]
        small_send[2, 8 + b : 9 + b, :] = crosses[b] + cross_local[b]
    small_exchange(2)
    sums = small_total(2)
    values1 = sums[0:4]
    coupled1 = coupled_rows(sums[0:8])[0:4]
    self_dots = band_dots(values1, coupled1)
    cross_dots = band_dots(values1, coupled0)
    weight0, weight1 = [], []
    for b in range(2):
        ratio = lane_total(sums[4 + b : 5 + b]) / norm0[b]
        self_curve = lane_total(sums[6 + b : 7 + b]) + self_dots[b]
        cross_curve = lane_total(sums[8 + b : 9 + b]) + cross_dots[b]
        curve = self_curve + ratio * (2.0 * cross_curve + ratio * curve0[b])
        alpha = lane_total(sums[4 + b : 5 + b]) / curve
        weight0.append(alpha0[b] + alpha * ratio)
        weight1.append(alpha)

    for p in range(PLANES):
        total = jnp.zeros((GRID, 128), f32)
        for b in range(2):
            lanes = slice(128 * (2 * p + b), 128 * (2 * p + b) + 128)
            for c in range(2):
                at = slice(96 * c, 96 * c + 96)
                change = weight0[b] * field0[at, lanes] + weight1[b] * field1[at, lanes]
                total = total + psi_field[at, lanes] * change
        dens[:, 128 * p : 128 * p + 128] = 4.0 * total
    for i in range(nb):
        part_send[i, 0:12, :] = dens[12 * i : 12 * i + 12, :]
        part_send[i, 12:16, :] = jnp.zeros((4, 768), f32)

    def part_out(k, c):
        part_copy(k, None).start()
        return c

    lax.fori_loop(1, nb, part_out, 0)
    part_recv[mb] = part_send[mb]
    for c in range(2):
        for b in range(2):
            at = slice(192 * c + 96 * b, 192 * c + 96 * b + 96)
            response[c, b] = weight0[b] * direction[at, :] + weight1[b] * residual[at, :]

    def part_in(k, c):
        part_copy(k, 0).wait_recv()
        return c

    lax.fori_loop(1, nb, part_in, 0)
    density[...] = jnp.sum(part_recv[...], axis=0)[0:12, :]

    def sent(k, c):
        for rnd in range(5):
            ga_copy(rnd, k).wait_send()
        for rnd in range(3):
            small_copy(rnd, k, None).wait_send()
        return c

    lax.fori_loop(1, GROUPS, sent, 0)

    def band_sent(k, c):
        psi_copy(k, None).wait_send()
        part_copy(k, None).wait_send()
        return c

    lax.fori_loop(1, nb, band_sent, 0)


def per_device(psi, vloc, dv, beta, dij, atom_type, stick_xy, band_shift):
    def padded(plane):
        cube = plane.reshape(PLANES, GRID, GRID)
        cube = jnp.pad(cube, ((0, 0), (0, 0), (0, 128 - GRID)))
        return jnp.moveaxis(cube, 0, 1).reshape(GRID, PLANES * 128)

    vmem = pl.BlockSpec(memory_space=pltpu.VMEM)
    smem = pl.BlockSpec(memory_space=pltpu.SMEM)
    dma = pltpu.SemaphoreType.DMA
    response, density = pl.pallas_call(
        kernel,
        out_shape=(
            jax.ShapeDtypeStruct((2, 2, GRID, 128), f32),
            jax.ShapeDtypeStruct((12, PLANES * 128), f32),
        ),
        in_specs=[smem, smem, vmem, vmem, vmem, pl.BlockSpec(memory_space=pl.ANY)] + [vmem] * 13,
        out_specs=(vmem, vmem),
        scratch_shapes=[
            pltpu.VMEM((2, 128, GRID, 128), f32),
            pltpu.VMEM((8, 2, 2, GRID, 128), bf16),
            pltpu.VMEM((256, 2048), bf16),
            pltpu.VMEM((16, 2048), f32),
            pltpu.VMEM((5, GROUPS, ROWS, 128), f32),
            pltpu.VMEM((5, GROUPS, ROWS, 128), f32),
            pltpu.VMEM((3, 16, 128), f32),
            pltpu.VMEM((3, GROUPS, 16, 128), f32),
            pltpu.VMEM((8, 16, 768), f32),
            pltpu.VMEM((8, 16, 768), f32),
            pltpu.VMEM((768, 2048), bf16),
            pltpu.VMEM((384, 256), f32),
            pltpu.VMEM((192, 512), bf16),
            pltpu.VMEM((192, 512), bf16),
            pltpu.VMEM((128, 1536), bf16),
            pltpu.VMEM((128, 1536), bf16),
            pltpu.VMEM((192, 1536), f32),
            pltpu.VMEM((192, 1536), f32),
            pltpu.VMEM((192, 1536), f32),
            pltpu.VMEM((768, 256), bf16),
            pltpu.VMEM((4, 128, 128), f32),
            pltpu.VMEM((4, 128, 128), f32),
            pltpu.VMEM((128, 128), f32),
            pltpu.VMEM((2, 384, 128), f32),
            pltpu.VMEM((384, 128), f32),
            pltpu.VMEM((GRID, 128), f32),
            pltpu.VMEM((8, 2048), f32),
            pltpu.VMEM((GRID, 768), f32),
            dma,
            dma((8,)),
            dma((8,)),
            dma((5, GROUPS)),
            dma((5, GROUPS)),
            dma((3, GROUPS)),
            dma((3, GROUPS)),
            dma((8,)),
            dma((8,)),
        ],
        compiler_params=pltpu.CompilerParams(
            collective_id=0, has_side_effects=True, vmem_limit_bytes=60 * 1024 * 1024
        ),
    )(
        band_shift,
        dij.reshape(32),
        psi,
        padded(vloc),
        padded(dv),
        beta,
        jnp.repeat(atom_type, 4).reshape(1, 128),
        stick_xy.reshape(1, 2048),
        *tables(2),
    )
    cells = density.reshape(12, PLANES, 128)[:, :, :GRID]
    return response, jnp.moveaxis(cells, 0, 1).reshape(PLANES, 12 * GRID)


def solution(mesh):
    return jax.shard_map(
        per_device,
        mesh=mesh,
        in_specs=(
            P(None, "band", None, "ga"),
            P("ga", None),
            P("ga", None),
            P(None, None, None, "ga"),
            P(),
            P(),
            P(),
            P("band"),
        ),
        out_specs=(P(None, "band", None, "ga"), P("ga", "band")),
        check_vma=False,
    )
```

profile of v0, /device:TPU:1, one launch (start us, length us, event | category | flops | bytes accessed | tf_op | source)
XLA Modules:
  0.0 94.9 jit_solution(16168395417099470423)
XLA Ops:
  0.6 1.1 %reshape.29 = f32[6,96,96]{2,1,0:T(8,128)S(1)} reshape(f32[6,9216]{1,0:T(8,128)} %param.20) | data formatting | bytes 442368 | tf_op jit(solution)/shard_map/reshape | solution.py:595
  1.7 0.2 copy.24
  2.0 1.1 %reshape.31 = f32[6,96,96]{2,1,0:T(8,128)S(1)} reshape(f32[6,9216]{1,0:T(8,128)} %param.21) | data formatting | bytes 442368 | tf_op jit(solution)/shard_map/reshape | solution.py:595
  3.0 0.2 copy.25
  3.3 0.9 copy_bitcast_fusion
  4.2 0.7 broadcast_in_dim.3
  4.9 0.6 reshape_reshape.3.kind
  5.5 1.3 %reshape.28.dij = f32[32]{0:T(128)} reshape(f32[2,4,4]{2,1,0:T(4,128)} %param.23) | data formatting | bytes 256 | tf_op jit(solution)/shard_map/reshape | solution.py:654
  6.8 84.9 %shard_map.194 = (f32[2,2,96,128]{3,2,1,0:T(8,128)}, f32[12,768]{1,0:T(8,128)}) custom-call(f32[2]{0:T(128)} %shift.1, f32[32]{0:T(128)} %reshape.28.dij, bf16[2,2,96,128]{3,2,1,0:T(8,128)(2,1)} %psi.1, f32[96,768]{1,0:T(8,128)} %get-tuple-element.7.vloc, f32[96,768]{1,0:T(8,128)} %get-tuple-element.6.dv, f32[2,128,96,128]{3,2,1,0:T(8,128)} %beta_hbm.1, ...), custom_call_target="tpu_custom_call" | custom-call | tf_op jit(solution)/shard_map/pallas_call | solution.py:602
  91.7 0.8 reshape.34
  92.6 0.7 reshape.35
  93.3 1.6 %copy.32 = f32[2,2,96,128]{3,2,1,0:T(8,128)} copy(f32[2,2,96,128]{3,2,1,0:T(8,128)} %get-tuple-element.10) | data formatting | bytes 393216
  (4 shorter events, 0.1 us)
where the time goes:
time: 95.2 us; the launch traced here: 94.9 us
  Pallas kernels  84.9 us (89%)
  local copies, waits for them, and re-layouts  9.3 us (10%)
    pallas_call x1, Pallas kernels, per_device(): pl.pallas_call(kernel, out_shape=(jax.ShapeDtypeStruct((2, 2, GRID, 128),...  84.9 us
    reshape x4, local copies, waits for them, and re-layouts, padded(): cube = plane.reshape(PLANES, GRID, GRID)  2.54 us

commit v1 on v0

--- a/solution.py
+++ b/solution.py
@@ -87,13 +87,15 @@
 
 
 def kernel(
-    shift, dij, psi, vloc, dv, beta_hbm, kind, sticks,
-    zh, zl, zth, ztl, xh, xl, xth, xtl, yh, yl, yt3,
+    shift, dij, kind, psi, sticks, zh, zl,
+    vloc_hbm, dv_hbm, zth_hbm, ztl_hbm, xh_hbm, xl_hbm, xth_hbm, xtl_hbm,
+    yh_hbm, yl_hbm, yt3_hbm, beta_hbm,
     response, density,
-    beta, occupied, onehot, mask, send, recv, small_send, small_recv,
+    vloc_flat, dv_flat, zth, ztl, xh, xl, xth, xtl, yh, yl, yt3,
+    beta, vloc, dv, cells, occupied, onehot, mask, send, recv, small_send, small_recv,
     part_send, part_recv, lhs, grid, eh, el, dh, dl, psi_field, field0, field1,
     q, proj, coef, couple, vec, image, kin, own, dens,
-    beta_sem, psi_ssem, psi_rsem, ssem, rsem, tssem, trsem, dssem, drsem,
+    load_sem, psi_ssem, psi_rsem, ssem, rsem, tssem, trsem, dssem, drsem,
 ):
     me = lax.axis_index("ga")
     mb = lax.axis_index("band")
@@ -115,8 +117,16 @@
 
     lax.fori_loop(1, GROUPS, greet_ga, 0)
     lax.fori_loop(1, nb, greet_band, 0)
-    beta_copy = pltpu.make_async_copy(beta_hbm, beta, beta_sem)
-    beta_copy.start()
+    loads = {}
+    pairs = dict(
+        dv=(dv_hbm, dv_flat), xh=(xh_hbm, xh), xl=(xl_hbm, xl), yh=(yh_hbm, yh),
+        yl=(yl_hbm, yl), yt3=(yt3_hbm, yt3), xth=(xth_hbm, xth), xtl=(xtl_hbm, xtl),
+        zth=(zth_hbm, zth), ztl=(ztl_hbm, ztl), vloc=(vloc_hbm, vloc_flat),
+        beta=(beta_hbm, beta),
+    )
+    for at, (name, (source, target)) in enumerate(pairs.items()):
+        loads[name] = pltpu.make_async_copy(source, target, load_sem.at[at])
+        loads[name].start()
 
     def ga_copy(rnd, k):
         other = lax.rem(me + k, GROUPS)
@@ -148,6 +158,7 @@
         lax.fori_loop(1, GROUPS, body, 0)
         recv[rnd, me] = send[rnd, me]
 
+    @jax.named_scope("arrived")
     def arrived(rnd):
         def body(k, c):
             ga_landed(rnd, k).wait_recv()
@@ -179,7 +190,8 @@
             small_copy(rnd, k, 0).wait_recv()
             return c
 
-        lax.fori_loop(1, GROUPS, body, 0)
+        with jax.named_scope("small_wait"):
+            lax.fori_loop(1, GROUPS, body, 0)
         return jnp.sum(small_recv[rnd], axis=0)
 
     def psi_copy(k, slot):
@@ -204,11 +216,14 @@
             device_id_type=MESH,
         )
 
-    wide = psi[...].reshape(384, 128)
-    send[0] = dot(
-        jnp.concatenate([zh[...], zl[...]], axis=1), jnp.concatenate([wide, wide], axis=0)
-    ).reshape(GROUPS, ROWS, 128)
-    pl.semaphore_wait(barrier, GROUPS - 1 + nb - 1)
+    with jax.named_scope("z_psi"):
+        wide = psi[...].reshape(384, 128)
+        send[0] = dot(
+            jnp.concatenate([zh[...], zl[...]], axis=1),
+            jnp.concatenate([wide, wide], axis=0),
+        ).reshape(GROUPS, ROWS, 128)
+    with jax.named_scope("barrier"):
+        pl.semaphore_wait(barrier, GROUPS - 1 + nb - 1)
     exchange(0)
 
     def psi_out(k, c):
@@ -226,46 +241,85 @@
         fx = jnp.where(x >= GRID // 2, x - GRID, x)
         return fy, fx
 
-    fy, fx = places(sticks[...])
-    ky = fy + SIDE // 2
-    kx = fx + SIDE // 2
-    high = jnp.floor(ky * 0.25)
-    low = (ky - 4.0 * high) * SIDE + kx
-    own[0:1, :] = low
-    own[1:2, :] = high
-    mask[...] = (
-        lax.broadcasted_iota(jnp.int32, (16, 2048), 0).astype(f32) == own[1:2, :]
-    ).astype(f32)
-
-    def fill(k, c):
-        lanes = pl.ds(pl.multiple_of(k * 256, 256), 256)
-        ids = lax.broadcasted_iota(jnp.int32, (256, 256), 0).astype(f32)
-        onehot[:, lanes] = (ids == own[0:1, lanes]).astype(f32).astype(bf16)
-        return c
-
-    lax.fori_loop(0, 8, fill, 0)
-    mine = sticks[:, pl.ds(pl.multiple_of(me * 128, 128), 128)]
-    oy, ox = places(mine)
-    kz = lax.broadcasted_iota(jnp.int32, (GRID, 128), 0).astype(f32)
-    fz = jnp.where(kz >= GRID // 2, kz - GRID, kz)
-    kin[...] = (fz * fz + (oy * oy + ox * ox)) * (4.0 / (GRID * GRID))
+    with jax.named_scope("tables"):
+        fy, fx = places(sticks[...])
+        ky = fy + SIDE // 2
+        kx = fx + SIDE // 2
+        high = jnp.floor(ky * 0.25)
+        low = (ky - 4.0 * high) * SIDE + kx
+        for k in range(GROUPS):
+            own[0:1, 128 * k : 128 * k + 128] = low[k : k + 1, :]
+            own[1:2, 128 * k : 128 * k + 128] = high[k : k + 1, :]
+        mask[...] = (
+            lax.broadcasted_iota(jnp.int32, (16, 2048), 0).astype(f32) == own[1:2, :]
+        ).astype(f32)
+
+        def fill(k, c):
+            lanes = pl.ds(pl.multiple_of(k * 256, 256), 256)
+            ids = lax.broadcasted_iota(jnp.int32, (256, 256), 0).astype(f32)
+            onehot[:, lanes] = (ids == own[0:1, lanes]).astype(f32).astype(bf16)
+            return c
+
+        lax.fori_loop(0, 8, fill, 0)
+        oy, ox = places(sticks[pl.ds(me, 1), :])
+        kz = lax.broadcasted_iota(jnp.int32, (GRID, 128), 0).astype(f32)
+        fz = jnp.where(kz >= GRID // 2, kz - GRID, kz)
+        kin[...] = (fz * fz + (oy * oy + ox * ox)) * (4.0 / (GRID * GRID))
 
     row = lax.broadcasted_iota(jnp.int32, (128, 128), 0)
     lane = lax.broadcasted_iota(jnp.int32, (128, 128), 1)
-    same = (row // 4) == (lane // 4)
-    first = kind[...] == 0
-    total = jnp.zeros((128, 128), f32)
-    for i in range(4):
-        for k in range(4):
-            value = jnp.where(first, dij[i * 4 + k], dij[16 + i * 4 + k])
-            here = same & ((row % 4) == i) & ((lane % 4) == k)
-            total = total + jnp.where(here, value, 0.0)
-    couple[...] = total
+
+    def couple_all():
+        atom = lax.broadcasted_iota(jnp.int32, (1, 128), 1) // 4
+        kinds = jnp.zeros((1, 128), jnp.int32)
+        for a in range(32):
+            kinds = jnp.where(atom == a, kind[a], kinds)
+        same = (row // 4) == (lane // 4)
+        first = kinds == 0
+        total = jnp.zeros((128, 128), f32)
+        for i in range(4):
+            for k in range(4):
+                value = jnp.where(first, dij[0, i, k], dij[1, i, k])
+                here = same & ((row % 4) == i) & ((lane % 4) == k)
+                total = total + jnp.where(here, value, 0.0)
+        couple[...] = total
+
+    def unpack(flat, out):
+        def body(g, c):
+            piece = flat[:, pl.ds(pl.multiple_of(g * 384, 384), 384)]
+            tail = jnp.zeros((PLANES, 32), f32)
+            for r in range(4):
+                if r < 3:
+                    cut = piece[:, 96 * r : 96 * r + 128]
+                else:
+                    cut = jnp.concatenate([piece[:, 288:384], tail], axis=1)
+                cells[pl.ds(pl.multiple_of(g * 32, 32) + 8 * r, PLANES), :] = cut
+            return c
+
+        lax.fori_loop(0, 24, body, 0)
+        for p in range(PLANES):
+            out[:, 128 * p : 128 * p + 128] = cells[pl.ds(p, GRID, stride=8), :]
+
+    with jax.named_scope("couple"):
+        couple_all()
+    with jax.named_scope("unpack"):
+        loads["dv"].wait()
+        unpack(dv_flat, dv)
+        loads["vloc"].wait()
+        unpack(vloc_flat, vloc)
+    for name in ("xh", "xl", "yh", "yl", "yt3", "xth", "xtl", "zth", "ztl"):
+        loads[name].wait()
     ones = jnp.ones((256, 128), bf16)
 
     def fill_planes(rnd, out):
 
-        def body(src, c):
+        def body(k, c):
+            src = lax.rem(me + k, GROUPS)
+
+            @pl.when(k > 0)
+            def _():
+                ga_landed(rnd, k).wait_recv()
+
             piece = recv[rnd, src]
             upper = piece.astype(bf16).astype(f32)
             lower = piece - upper
@@ -280,84 +334,119 @@
                 ).astype(bf16)
             return c
 
-        lax.fori_loop(0, GROUPS, body, 0)
-        both = dot_nt(lhs[...], onehot[...])
-        grid[...] = both[0:384] + both[384:768]
-        for t in range(2):
-            lanes = slice(128 * t, 128 * t + 128)
-            data = jnp.concatenate([grid[0:192, lanes], grid[192:384, lanes]], axis=1)
-            ah, al = split(data)
-            along = right(ah, al, xh[...], xl[...])
-            uh, ul = split(along)
-            eh[...] = uh
-            el[...] = ul
-            for c in range(2):
-                for j in range(2):
-                    rows = slice(16 * (4 * c + 2 * t + j), 16 * (4 * c + 2 * t + j) + 16)
-                    cols = slice(128 * (2 * c + j), 128 * (2 * c + j) + 128)
-                    for i in range(12):
-                        dh[rows, 128 * i : 128 * i + 128] = eh[16 * i : 16 * i + 16, cols]
-                        dl[rows, 128 * i : 128 * i + 128] = el[16 * i : 16 * i + 16, cols]
-        for part in range(6):
-            lanes = slice(256 * part, 256 * part + 256)
-            out[:, lanes] = dot(
-                jnp.concatenate([yh[...], yh[...], yl[...]], axis=1),
-                jnp.concatenate([dh[:, lanes], dl[:, lanes], dh[:, lanes]], axis=0),
-            )
+        with jax.named_scope("fill_lhs"):
+            lax.fori_loop(0, GROUPS, body, 0)
+        with jax.named_scope("fill_dot"):
+            both = dot_nt(lhs[...], onehot[...])
+            grid[...] = both[0:384] + both[384:768]
+        with jax.named_scope("fill_x"):
+            for t in range(2):
+                lanes = slice(128 * t, 128 * t + 128)
+                data = jnp.concatenate([grid[0:192, lanes], grid[192:384, lanes]], axis=1)
+                ah, al = split(data)
+                along = right(ah, al, xh[...], xl[...])
+                uh, ul = split(along)
+                eh[...] = uh
+                el[...] = ul
+                for c in range(2):
+                    for j in range(2):
+                        rows = slice(16 * (4 * c + 2 * t + j), 16 * (4 * c + 2 * t + j) + 16)
+                        cols = slice(128 * (2 * c + j), 128 * (2 * c + j) + 128)
+                        for i in range(12):
+                            dh[rows, 128 * i : 128 * i + 128] = eh[16 * i : 16 * i + 16, cols]
+                            dl[rows, 128 * i : 128 * i + 128] = el[16 * i : 16 * i + 16, cols]
+        with jax.named_scope("fill_y"):
+            for part in range(6):
+                lanes = slice(256 * part, 256 * part + 256)
+                out[:, lanes] = dot(
+                    jnp.concatenate([yh[...], yh[...], yl[...]], axis=1),
+                    jnp.concatenate([dh[:, lanes], dl[:, lanes], dh[:, lanes]], axis=0),
+                )
 
     def to_sticks(rnd, potential, source):
-        for p in range(PLANES):
-            lanes = slice(256 * p, 256 * p + 256)
-            pot = potential[:, 128 * p : 128 * p + 128]
-            pot = jnp.concatenate([pot, pot], axis=1)
-            pot = jnp.concatenate([pot, pot], axis=0)
-            ah, al = split(source[:, lanes] * pot)
-            along = dot(yt3[...], jnp.concatenate([ah, al, ah], axis=0))
-            uh, ul = split(along)
-            dh[:, lanes] = uh
-            dl[:, lanes] = ul
-        for t in range(2):
-            for c in range(2):
-                for j in range(2):
-                    rows = slice(16 * (4 * c + 2 * t + j), 16 * (4 * c + 2 * t + j) + 16)
-                    cols = slice(128 * (2 * c + j), 128 * (2 * c + j) + 128)
-                    for i in range(12):
-                        eh[16 * i : 16 * i + 16, cols] = dh[rows, 128 * i : 128 * i + 128]
-                        el[16 * i : 16 * i + 16, cols] = dl[rows, 128 * i : 128 * i + 128]
-            along = right(eh[...], el[...], xth[...], xtl[...])
-            uh, ul = split(along)
-            lanes = slice(128 * t, 128 * t + 128)
-            for c in range(2):
-                q[192 * c : 192 * c + 192, lanes] = uh[:, 128 * c : 128 * c + 128]
-                q[384 + 192 * c : 576 + 192 * c, lanes] = ul[:, 128 * c : 128 * c + 128]
+        with jax.named_scope("stick_y"):
+            for p in range(PLANES):
+                lanes = slice(256 * p, 256 * p + 256)
+                pot = potential[:, 128 * p : 128 * p + 128]
+                pot = jnp.concatenate([pot, pot], axis=1)
+                pot = jnp.concatenate([pot, pot], axis=0)
+                ah, al = split(source[:, lanes] * pot)
+                along = dot(yt3[...], jnp.concatenate([ah, al, ah], axis=0))
+                uh, ul = split(along)
+                dh[:, lanes] = uh
+                dl[:, lanes] = ul
+        with jax.named_scope("stick_x"):
+            for t in range(2):
+                for c in range(2):
+                    for j in range(2):
+                        rows = slice(16 * (4 * c + 2 * t + j), 16 * (4 * c + 2 * t + j) + 16)
+                        cols = slice(128 * (2 * c + j), 128 * (2 * c + j) + 128)
+                        for i in range(12):
+                            eh[16 * i : 16 * i + 16, cols] = dh[rows, 128 * i : 128 * i + 128]
+                            el[16 * i : 16 * i + 16, cols] = dl[rows, 128 * i : 128 * i + 128]
+                along = right(eh[...], el[...], xth[...], xtl[...])
+                uh, ul = split(along)
+                lanes = slice(128 * t, 128 * t + 128)
+                for c in range(2):
+                    q[192 * c : 192 * c + 192, lanes] = uh[:, 128 * c : 128 * c + 128]
+                    q[384 + 192 * c : 576 + 192 * c, lanes] = ul[:, 128 * c : 128 * c + 128]
 
         def body(k, carry):
-            lanes = pl.ds(pl.multiple_of(k * 256, 256), 256)
+            pair = lax.rem(me // 2 + k, 8)
+            lanes = pl.ds(pl.multiple_of(pair * 256, 256), 256)
             place = onehot[:, lanes]
             keep = mask[:, lanes]
             both = dot(q[...], place)
             found = both[0:384] + both[384:768]
             picked = jnp.sum(found.reshape(ROWS, 16, 256) * keep[None], axis=1)
-            send[rnd, 2 * k] = picked[:, 0:128]
-            send[rnd, 2 * k + 1] = picked[:, 128:256]
+            send[rnd, 2 * pair] = picked[:, 0:128]
+            send[rnd, 2 * pair + 1] = picked[:, 128:256]
+
+            @pl.when(k > 0)
+            def _():
+                post(rnd, lax.rem(me // 2 + k + 7, 8))
+
             return carry
 
-        lax.fori_loop(0, 8, body, 0)
+        with jax.named_scope("stick_pick"):
+            lax.fori_loop(0, 8, body, 0)
+            post(rnd, lax.rem(me // 2 + 7, 8))
+            recv[rnd, me] = send[rnd, me]
+
+    def post(rnd, pair):
+        for half in range(2):
+            owner = 2 * pair + half
+
+            @pl.when(owner != me)
+            def _():
+                ga_copy(rnd, owner - me + GROUPS).start()
 
     def z_forward(rnd):
         return left(zth[...], ztl[...], recv[rnd].reshape(384, 128))
 
     def project(load, count, source):
-        def body(j, c):
-            p0, p1 = load(j)
-            for b in range(2):
-                v0 = source[96 * b : 96 * b + 96, :]
-                v1 = source[192 + 96 * b : 288 + 96 * b, :]
-                proj[b, pl.ds(j, 1), :] = row_sum(p0 * v0 + p1 * v1)
-                proj[2 + b, pl.ds(j, 1), :] = row_sum(p0 * v1 - p1 * v0)
+        step = 4
+
+        def body(g, c):
+            sums = [[None] * 4 for _ in range(step)]
+            for z in range(GRID // 8):
+                v = [source[96 * n + 8 * z : 96 * n + 8 * z + 8, :] for n in range(4)]
+                for t in range(step):
+                    p0, p1 = load(g * step + t, 8 * z, 8)
+                    for b in range(2):
+                        re = p0 * v[b] + p1 * v[2 + b]
+                        im = p0 * v[2 + b] - p1 * v[b]
+                        sums[t][b] = re if z == 0 else sums[t][b] + re
+                        sums[t][2 + b] = im if z == 0 else sums[t][2 + b] + im
+            for t in range(step):
+                for o in range(4):
+                    proj[o, pl.ds(g * step + t, 1), :] = jnp.sum(
+                        sums[t][o], axis=0, keepdims=True
+                    )
             return c
 
-        lax.fori_loop(0, count, body, 0)
+        with jax.named_scope("project"):
+            lax.fori_loop(0, count // step, body, 0)
 
     def projections(o, count):
         ph, pl_ = split(proj[o, 0:count, :])
@@ -376,22 +465,26 @@
         rows = 24
         for z in range(GRID // rows):
 
-            def body(j, acc):
-                p0, p1 = load(j, z * rows, rows)
-                out = []
-                for b in range(2):
-                    cr = coef[b, pl.ds(j, 1), :]
-                    ci = coef[2 + b, pl.ds(j, 1), :]
-                    out.append(acc[2 * b] + (p0 * cr - p1 * ci))
-                    out.append(acc[2 * b + 1] + (p0 * ci + p1 * cr))
-                return tuple(out)
+            def body(g, acc):
+                for t in range(4):
+                    j = g * 4 + t
+                    p0, p1 = load(j, z * rows, rows)
+                    out = []
+                    for b in range(2):
+                        cr = coef[b, pl.ds(j, 1), :]
+                        ci = coef[2 + b, pl.ds(j, 1), :]
+                        out.append(acc[2 * b] + (p0 * cr - p1 * ci))
+                        out.append(acc[2 * b + 1] + (p0 * ci + p1 * cr))
+                    acc = out
+                return tuple(acc)
 
             init = tuple(
                 base[192 * c + 96 * b + z * rows : 192 * c + 96 * b + z * rows + rows, :]
                 for b in range(2)
                 for c in range(2)
             )
-            done = lax.fori_loop(0, count, body, init)
+            with jax.named_scope("apply"):
+                done = lax.fori_loop(0, count // 4, body, init)
             for b in range(2):
                 for c in range(2):
                     at = 192 * c + 96 * b + z * rows
@@ -407,10 +500,8 @@
             occupied[owner, 1, b, at : at + rows, :].astype(f32),
         )
 
-    arrived(0)
     fill_planes(0, psi_field)
     to_sticks(1, dv, psi_field)
-    exchange(1)
 
     def psi_in(k, c):
         psi_copy(k, 0).wait_recv()
@@ -421,7 +512,7 @@
     lax.fori_loop(1, nb, psi_in, 0)
 
     project(psi_rows, 16, vec.at[1])
-    small_send[0] = jnp.zeros((16, 128), f32)
+    small_send[0] = jnp.zeros((8, 128), f32)
     for o in range(4):
         small_send[0, o : o + 1, 0:16] = projections(o, 16)
     small_exchange(0)
@@ -459,6 +550,18 @@
             out.append(total)
         return out
 
+    half = lax.broadcasted_iota(jnp.int32, (1, 128), 1) < 64
+
+    def packed(pair):
+        a, b = (r + pltpu.roll(r, 64, 1) for r in pair)
+        return jnp.where(half, a, b)
+
+    def unpacked(both):
+        return [
+            lane_total(jnp.where(half, both, 0.0)),
+            lane_total(jnp.where(half, 0.0, both)),
+        ]
+
     def band_dots(values, coupled):
         both = values * coupled
         return [lane_total(both[b : b + 1] + both[2 + b : 3 + b]) for b in range(2)]
@@ -473,28 +576,25 @@
 
     direction = vec.at[0]
     transform_out(2, direction)
-    beta_copy.wait()
+    loads["beta"].wait()
     project(beta_rows, 128, direction)
-    small_send[1] = jnp.zeros((16, 128), f32)
+    small_send[1] = jnp.zeros((8, 128), f32)
     for o in range(4):
         small_send[1, o : o + 1, :] = projections(o, 128)
     norms = stick_sum(direction, direction)
     curves = stick_sum(direction, direction, True)
-    arrived(2)
     fill_planes(2, field0)
     local = grid_sum(field0, field0)
-    for b in range(2):
-        small_send[1, 4 + b : 5 + b, :] = norms[b]
-        small_send[1, 6 + b : 7 + b, :] = curves[b] + local[b]
+    small_send[1, 4:5, :] = packed(norms)
+    small_send[1, 5:6, :] = packed([curves[b] + local[b] for b in range(2)])
     small_exchange(1)
     to_sticks(3, vloc, field0)
-    exchange(3)
     sums = small_total(1)
     values0 = sums[0:4]
-    coupled0 = coupled_rows(sums[0:8])[0:4]
+    coupled0 = coupled_rows(sums)[0:4]
     nonlocal0 = band_dots(values0, coupled0)
-    norm0 = [lane_total(sums[4 + b : 5 + b]) for b in range(2)]
-    curve0 = [lane_total(sums[6 + b : 7 + b]) + nonlocal0[b] for b in range(2)]
+    norm0 = unpacked(sums[4:5])
+    curve0 = [c + n for c, n in zip(unpacked(sums[5:6]), nonlocal0)]
     alpha0 = [norm0[b] / curve0[b] for b in range(2)]
     spread(couple[...], values0)
     for c in range(2):
@@ -512,48 +612,52 @@
 
     transform_out(4, residual)
     project(beta_rows, 128, residual)
-    small_send[2] = jnp.zeros((16, 128), f32)
+    small_send[2] = jnp.zeros((8, 128), f32)
     for o in range(4):
         small_send[2, o : o + 1, :] = projections(o, 128)
     norms = stick_sum(residual, residual)
     selfs = stick_sum(residual, residual, True)
     crosses = stick_sum(residual, direction, True)
-    arrived(4)
     fill_planes(4, field1)
     self_local = grid_sum(field1, field1)
     cross_local = grid_sum(field1, field0)
-    for b in range(2):
-        small_send[2, 4 + b : 5 + b, :] = norms[b]
-        small_send[2, 6 + b : 7 + b, :] = selfs[b] + self_local[b]
-        small_send[2, 8 + b : 9 + b, :] = crosses[b] + cross_local[b]
+    small_send[2, 4:5, :] = packed(norms)
+    small_send[2, 5:6, :] = packed([selfs[b] + self_local[b] for b in range(2)])
+    small_send[2, 6:7, :] = packed([crosses[b] + cross_local[b] for b in range(2)])
     small_exchange(2)
+    with jax.named_scope("products"):
+        for p in range(PLANES):
+            for b in range(2):
+                lanes = slice(128 * (2 * p + b), 128 * (2 * p + b) + 128)
+                for n, field in enumerate((field0, field1)):
+                    dens[96 * n : 96 * n + 96, lanes] = 4.0 * (
+                        psi_field[0:96, lanes] * field[0:96, lanes]
+                        + psi_field[96:192, lanes] * field[96:192, lanes]
+                    )
     sums = small_total(2)
     values1 = sums[0:4]
-    coupled1 = coupled_rows(sums[0:8])[0:4]
+    coupled1 = coupled_rows(sums)[0:4]
     self_dots = band_dots(values1, coupled1)
     cross_dots = band_dots(values1, coupled0)
     weight0, weight1 = [], []
+    norm1, self1, cross1 = (unpacked(sums[n : n + 1]) for n in (4, 5, 6))
     for b in range(2):
-        ratio = lane_total(sums[4 + b : 5 + b]) / norm0[b]
-        self_curve = lane_total(sums[6 + b : 7 + b]) + self_dots[b]
-        cross_curve = lane_total(sums[8 + b : 9 + b]) + cross_dots[b]
+        ratio = norm1[b] / norm0[b]
+        self_curve = self1[b] + self_dots[b]
+        cross_curve = cross1[b] + cross_dots[b]
         curve = self_curve + ratio * (2.0 * cross_curve + ratio * curve0[b])
-        alpha = lane_total(sums[4 + b : 5 + b]) / curve
+        alpha = norm1[b] / curve
         weight0.append(alpha0[b] + alpha * ratio)
         weight1.append(alpha)
 
-    for p in range(PLANES):
-        total = jnp.zeros((GRID, 128), f32)
-        for b in range(2):
-            lanes = slice(128 * (2 * p + b), 128 * (2 * p + b) + 128)
-            for c in range(2):
-                at = slice(96 * c, 96 * c + 96)
-                change = weight0[b] * field0[at, lanes] + weight1[b] * field1[at, lanes]
-                total = total + psi_field[at, lanes] * change
-        dens[:, 128 * p : 128 * p + 128] = 4.0 * total
-    for i in range(nb):
-        part_send[i, 0:12, :] = dens[12 * i : 12 * i + 12, :]
-        part_send[i, 12:16, :] = jnp.zeros((4, 768), f32)
+    with jax.named_scope("density"):
+        for p in range(PLANES):
+            total = jnp.zeros((GRID, 128), f32)
+            for b in range(2):
+                lanes = slice(128 * (2 * p + b), 128 * (2 * p + b) + 128)
+                total = total + weight0[b] * dens[0:96, lanes] + weight1[b] * dens[96:192, lanes]
+            for i in range(nb):
+                part_send[i, 12 * p : 12 * p + 12, :] = total[12 * i : 12 * i + 12, :]
 
     def part_out(k, c):
         part_copy(k, None).start()
@@ -570,8 +674,11 @@
         part_copy(k, 0).wait_recv()
         return c
 
-    lax.fori_loop(1, nb, part_in, 0)
-    density[...] = jnp.sum(part_recv[...], axis=0)[0:12, :]
+    with jax.named_scope("part_wait"):
+        lax.fori_loop(1, nb, part_in, 0)
+    cells[0:72, :] = jnp.sum(part_recv[...], axis=0)
+    for y in range(12):
+        density[:, 96 * y : 96 * y + 96] = cells[pl.ds(y, PLANES, stride=12), :][:, 0:96]
 
     def sent(k, c):
         for rnd in range(5):
@@ -591,33 +698,36 @@
 
 
 def per_device(psi, vloc, dv, beta, dij, atom_type, stick_xy, band_shift):
-    def padded(plane):
-        cube = plane.reshape(PLANES, GRID, GRID)
-        cube = jnp.pad(cube, ((0, 0), (0, 0), (0, 128 - GRID)))
-        return jnp.moveaxis(cube, 0, 1).reshape(GRID, PLANES * 128)
-
     vmem = pl.BlockSpec(memory_space=pltpu.VMEM)
     smem = pl.BlockSpec(memory_space=pltpu.SMEM)
     dma = pltpu.SemaphoreType.DMA
+    every = tables(2)
+    early, late = every[:2], every[2:]
     response, density = pl.pallas_call(
         kernel,
         out_shape=(
             jax.ShapeDtypeStruct((2, 2, GRID, 128), f32),
-            jax.ShapeDtypeStruct((12, PLANES * 128), f32),
+            jax.ShapeDtypeStruct((PLANES, 12 * GRID), f32),
         ),
-        in_specs=[smem, smem, vmem, vmem, vmem, pl.BlockSpec(memory_space=pl.ANY)] + [vmem] * 13,
+        in_specs=[smem] * 3 + [vmem] * 4 + [pl.BlockSpec(memory_space=pl.ANY)] * 12,
         out_specs=(vmem, vmem),
         scratch_shapes=[
+            pltpu.VMEM((PLANES, GRID * GRID), f32),
+            pltpu.VMEM((PLANES, GRID * GRID), f32),
+            *[pltpu.VMEM(t.shape, t.dtype) for t in late],
             pltpu.VMEM((2, 128, GRID, 128), f32),
+            pltpu.VMEM((GRID, 768), f32),
+            pltpu.VMEM((GRID, 768), f32),
+            pltpu.VMEM((768, 128), f32),
             pltpu.VMEM((8, 2, 2, GRID, 128), bf16),
             pltpu.VMEM((256, 2048), bf16),
             pltpu.VMEM((16, 2048), f32),
             pltpu.VMEM((5, GROUPS, ROWS, 128), f32),
             pltpu.VMEM((5, GROUPS, ROWS, 128), f32),
-            pltpu.VMEM((3, 16, 128), f32),
-            pltpu.VMEM((3, GROUPS, 16, 128), f32),
-            pltpu.VMEM((8, 16, 768), f32),
-            pltpu.VMEM((8, 16, 768), f32),
+            pltpu.VMEM((3, 8, 128), f32),
+            pltpu.VMEM((3, GROUPS, 8, 128), f32),
+            pltpu.VMEM((8, 72, 128), f32),
+            pltpu.VMEM((8, 72, 128), f32),
             pltpu.VMEM((768, 2048), bf16),
             pltpu.VMEM((384, 256), f32),
             pltpu.VMEM((192, 512), bf16),
@@ -635,8 +745,8 @@
             pltpu.VMEM((384, 128), f32),
             pltpu.VMEM((GRID, 128), f32),
             pltpu.VMEM((8, 2048), f32),
-            pltpu.VMEM((GRID, 768), f32),
-            dma,
+            pltpu.VMEM((192, 1536), f32),
+            dma((12,)),
             dma((8,)),
             dma((8,)),
             dma((5, GROUPS)),
@@ -650,18 +760,10 @@
             collective_id=0, has_side_effects=True, vmem_limit_bytes=60 * 1024 * 1024
         ),
     )(
-        band_shift,
-        dij.reshape(32),
-        psi,
-        padded(vloc),
-        padded(dv),
-        beta,
-        jnp.repeat(atom_type, 4).reshape(1, 128),
-        stick_xy.reshape(1, 2048),
-        *tables(2),
+        band_shift, dij, atom_type, psi, stick_xy.reshape(GROUPS, 128), *early,
+        vloc, dv, *late, beta,
     )
-    cells = density.reshape(12, PLANES, 128)[:, :, :GRID]
-    return response, jnp.moveaxis(cells, 0, 1).reshape(PLANES, 12 * GRID)
+    return response, density
 
 
 def solution(mesh):

time: 95.2 us -> 81 us (0.85)
  Pallas kernels: 84.9 us -> 77.1 us
  local copies, waits for them, and re-layouts: 9.3 us -> 3 us
    pallas_call x1, Pallas kernels: 84.9 us -> 77.1 us  [per_device(): pl.pallas_call(kernel, out_shape=(jax.ShapeDtypeStruct((2, 2, GRID, 128),...]
    reshape x8 -> x0, local copies, waits for them, and re-layouts: 6.25 us -> none  [the longest x4 2.54 us: padded(): cube = plane.reshape(PLANES, GRID, GRID)]
    unnamed x1 -> x2, local copies, waits for them, and re-layouts: 1.62 us -> 3 us
where the time goes in v1:
time: 81 us; the launch traced here: 80.8 us
  Pallas kernels  77.1 us (95%)
  local copies, waits for them, and re-layouts  3 us (4%)
    pallas_call x1, Pallas kernels, per_device(): pl.pallas_call(kernel, out_shape=(jax.ShapeDtypeStruct((2, 2, GRID, 128),...  77.1 us
    unnamed x2, local copies, waits for them, and re-layouts  3 us

profile of v1, /device:TPU:1, one launch (start us, length us, event | category | flops | bytes accessed | tf_op | source)
XLA Modules:
  0.0 80.8 jit_solution(8129461290830050880)
XLA Ops:
  0.6 77.1 %shard_map.194 = (f32[2,2,96,128]{3,2,1,0:T(8,128)}, f32[6,1152]{1,0:T(8,128)}) custom-call(f32[2]{0:T(128)} %shift.1, f32[2,4,4]{2,1,0:T(4,128)} %dij.1, s32[32]{0:T(128)} %kind.1, bf16[2,2,96,128]{3,2,1,0:T(8,128)(2,1)} %psi.1, s32[16,128]{1,0:T(8,128)} %bitcast.1, bf16[384,384]{1,0:T(8,128)(2,1)} %constant.22.clone.zh, ...), custom_call_target="tpu_custom_call" | custom-call | tf_op jit(solution)/shard_map/pallas_call | solution.py:706
  77.8 1.6 %copy.23 = f32[2,2,96,128]{3,2,1,0:T(8,128)} copy(f32[2,2,96,128]{3,2,1,0:T(8,128)} %get-tuple-element.4) | data formatting | bytes 393216
  79.4 1.4 %copy.24 = f32[6,1152]{1,0:T(8,128)} copy(f32[6,1152]{1,0:T(8,128)} %get-tuple-element.5) | data formatting | bytes 55296

commit v2 on v1

--- a/solution.py
+++ b/solution.py
@@ -42,7 +42,7 @@
     along_x[..., :GRID] = complex_table(unit * (freqs[:, None] * cells[None, :] % GRID))
     x_table = np.einsum("oikx,be->ibkoex", along_x, np.eye(2)).reshape(256, 512)
     along_y = complex_table(unit * (cells[:, None] * freqs[None, :] % GRID))
-    along_y = along_y.reshape(2, 2, GRID, 16, 4)
+    along_y = along_y.reshape(2, 2, GRID, 8, 8)
     y_table = np.einsum("oiygl->oyilg", along_y).reshape(192, 128)
     out = []
     for table in (z_table, z_table.T, x_table, x_table.T, y_table):
@@ -87,13 +87,12 @@
 
 
 def kernel(
-    shift, dij, kind, psi, sticks, zh, zl,
-    vloc_hbm, dv_hbm, zth_hbm, ztl_hbm, xh_hbm, xl_hbm, xth_hbm, xtl_hbm,
+    shift, dij, kind, psi_hbm, sticks_hbm, zh_hbm, zl_hbm, vloc_hbm, dv_hbm, zth_hbm, ztl_hbm, xh_hbm, xl_hbm, xth_hbm, xtl_hbm,
     yh_hbm, yl_hbm, yt3_hbm, beta_hbm,
-    response, density,
-    vloc_flat, dv_flat, zth, ztl, xh, xl, xth, xtl, yh, yl, yt3,
+    first_out, second_out, weights_out, cells_out,
+    psi, sticks, zh, zl, vloc_flat, dv_flat, zth, ztl, xh, xl, xth, xtl, yh, yl, yt3,
     beta, vloc, dv, cells, occupied, onehot, mask, send, recv, small_send, small_recv,
-    part_send, part_recv, lhs, grid, eh, el, dh, dl, psi_field, field0, field1,
+    part_send, part_recv, lhs, grid, ex, eh, el, dh, dl, psi_field, field0, field1,
     q, proj, coef, couple, vec, image, kin, own, dens,
     load_sem, psi_ssem, psi_rsem, ssem, rsem, tssem, trsem, dssem, drsem,
 ):
@@ -119,6 +118,7 @@
     lax.fori_loop(1, nb, greet_band, 0)
     loads = {}
     pairs = dict(
+        psi=(psi_hbm, psi), zh=(zh_hbm, zh), zl=(zl_hbm, zl), sticks=(sticks_hbm, sticks),
         dv=(dv_hbm, dv_flat), xh=(xh_hbm, xh), xl=(xl_hbm, xl), yh=(yh_hbm, yh),
         yl=(yl_hbm, yl), yt3=(yt3_hbm, yt3), xth=(xth_hbm, xth), xtl=(xtl_hbm, xtl),
         zth=(zth_hbm, zth), ztl=(ztl_hbm, ztl), vloc=(vloc_hbm, vloc_flat),
@@ -216,23 +216,14 @@
             device_id_type=MESH,
         )
 
+    for name in ("psi", "zh", "zl"):
+        loads[name].wait()
     with jax.named_scope("z_psi"):
         wide = psi[...].reshape(384, 128)
         send[0] = dot(
             jnp.concatenate([zh[...], zl[...]], axis=1),
             jnp.concatenate([wide, wide], axis=0),
         ).reshape(GROUPS, ROWS, 128)
-    with jax.named_scope("barrier"):
-        pl.semaphore_wait(barrier, GROUPS - 1 + nb - 1)
-    exchange(0)
-
-    def psi_out(k, c):
-        psi_copy(k, None).start()
-        return c
-
-    lax.fori_loop(1, nb, psi_out, 0)
-    occupied[mb] = psi[...]
-
     def places(xy):
         flat = xy.astype(f32)
         y = jnp.floor((flat + 0.5) * (1.0 / GRID))
@@ -241,22 +232,23 @@
         fx = jnp.where(x >= GRID // 2, x - GRID, x)
         return fy, fx
 
+    loads["sticks"].wait()
     with jax.named_scope("tables"):
         fy, fx = places(sticks[...])
         ky = fy + SIDE // 2
         kx = fx + SIDE // 2
-        high = jnp.floor(ky * 0.25)
-        low = (ky - 4.0 * high) * SIDE + kx
+        high = jnp.floor(ky * 0.125)
+        low = (ky - 8.0 * high) * SIDE + kx
         for k in range(GROUPS):
             own[0:1, 128 * k : 128 * k + 128] = low[k : k + 1, :]
             own[1:2, 128 * k : 128 * k + 128] = high[k : k + 1, :]
         mask[...] = (
-            lax.broadcasted_iota(jnp.int32, (16, 2048), 0).astype(f32) == own[1:2, :]
+            lax.broadcasted_iota(jnp.int32, (8, 2048), 0).astype(f32) == own[1:2, :]
         ).astype(f32)
 
         def fill(k, c):
             lanes = pl.ds(pl.multiple_of(k * 256, 256), 256)
-            ids = lax.broadcasted_iota(jnp.int32, (256, 256), 0).astype(f32)
+            ids = lax.broadcasted_iota(jnp.int32, (512, 256), 0).astype(f32)
             onehot[:, lanes] = (ids == own[0:1, lanes]).astype(f32).astype(bf16)
             return c
 
@@ -302,11 +294,20 @@
 
     with jax.named_scope("couple"):
         couple_all()
+    with jax.named_scope("barrier"):
+        pl.semaphore_wait(barrier, GROUPS - 1 + nb - 1)
+    exchange(0)
+
+    def psi_out(k, c):
+        psi_copy(k, None).start()
+        return c
+
+    lax.fori_loop(1, nb, psi_out, 0)
+    occupied[mb] = psi[...]
+
     with jax.named_scope("unpack"):
         loads["dv"].wait()
         unpack(dv_flat, dv)
-        loads["vloc"].wait()
-        unpack(vloc_flat, vloc)
     for name in ("xh", "xl", "yh", "yl", "yt3", "xth", "xtl", "zth", "ztl"):
         loads[name].wait()
     ones = jnp.ones((256, 128), bf16)
@@ -325,36 +326,37 @@
             lower = piece - upper
             cols = pl.ds(pl.multiple_of(src * 128, 128), 128)
             keep = mask[:, cols]
-            for r in range(ROWS):
-                lhs[16 * r : 16 * r + 16, cols] = (
-                    jnp.broadcast_to(upper[r : r + 1], (16, 128)) * keep
-                ).astype(bf16)
-                lhs[384 + 16 * r : 400 + 16 * r, cols] = (
-                    jnp.broadcast_to(lower[r : r + 1], (16, 128)) * keep
-                ).astype(bf16)
+            for n, part in enumerate((upper, lower)):
+                for r in range(0, ROWS, 2):
+                    two = [jnp.broadcast_to(part[r + e : r + e + 1], (8, 128)) * keep for e in (0, 1)]
+                    at = 192 * n + 8 * r
+                    lhs[at : at + 16, cols] = jnp.concatenate(two, axis=0).astype(bf16)
             return c
 
         with jax.named_scope("fill_lhs"):
             lax.fori_loop(0, GROUPS, body, 0)
         with jax.named_scope("fill_dot"):
             both = dot_nt(lhs[...], onehot[...])
-            grid[...] = both[0:384] + both[384:768]
+            grid[...] = both[0:192] + both[192:384]
         with jax.named_scope("fill_x"):
-            for t in range(2):
-                lanes = slice(128 * t, 128 * t + 128)
-                data = jnp.concatenate([grid[0:192, lanes], grid[192:384, lanes]], axis=1)
-                ah, al = split(data)
-                along = right(ah, al, xh[...], xl[...])
-                uh, ul = split(along)
-                eh[...] = uh
-                el[...] = ul
-                for c in range(2):
-                    for j in range(2):
-                        rows = slice(16 * (4 * c + 2 * t + j), 16 * (4 * c + 2 * t + j) + 16)
-                        cols = slice(128 * (2 * c + j), 128 * (2 * c + j) + 128)
-                        for i in range(12):
-                            dh[rows, 128 * i : 128 * i + 128] = eh[16 * i : 16 * i + 16, cols]
-                            dl[rows, 128 * i : 128 * i + 128] = el[16 * i : 16 * i + 16, cols]
+            data = [
+                jnp.concatenate(
+                    [grid[0:96, 128 * t : 128 * t + 128], grid[96:192, 128 * t : 128 * t + 128]],
+                    axis=1,
+                )
+                for t in range(4)
+            ]
+            ah, al = split(jnp.concatenate(data, axis=0))
+            ex[...] = right(ah, al, xh[...], xl[...])
+            for c in range(2):
+                for t in range(4):
+                    rows = slice(16 * (4 * c + t), 16 * (4 * c + t) + 16)
+                    for i in range(12):
+                        at = 96 * t + 8 * i
+                        two = [ex[at : at + 8, 128 * (2 * c + j) : 128 * (2 * c + j) + 128] for j in (0, 1)]
+                        uh, ul = split(jnp.concatenate(two, axis=0))
+                        dh[rows, 128 * i : 128 * i + 128] = uh
+                        dl[rows, 128 * i : 128 * i + 128] = ul
         with jax.named_scope("fill_y"):
             for part in range(6):
                 lanes = slice(256 * part, 256 * part + 256)
@@ -372,50 +374,43 @@
                 pot = jnp.concatenate([pot, pot], axis=0)
                 ah, al = split(source[:, lanes] * pot)
                 along = dot(yt3[...], jnp.concatenate([ah, al, ah], axis=0))
-                uh, ul = split(along)
-                dh[:, lanes] = uh
-                dl[:, lanes] = ul
+                for c in range(2):
+                    for t in range(4):
+                        for j in range(2):
+                            rows = slice(8 * (8 * c + 2 * t + j), 8 * (8 * c + 2 * t + j) + 8)
+                            two = jnp.concatenate([along[rows, 0:128], along[rows, 128:256]], axis=0)
+                            uh, ul = split(two)
+                            at = 96 * t + 16 * p
+                            cols = slice(128 * (2 * c + j), 128 * (2 * c + j) + 128)
+                            eh[at : at + 16, cols] = uh
+                            el[at : at + 16, cols] = ul
         with jax.named_scope("stick_x"):
-            for t in range(2):
+            along = right(eh[...], el[...], xth[...], xtl[...])
+            uh, ul = split(along)
+            for t in range(4):
                 for c in range(2):
-                    for j in range(2):
-                        rows = slice(16 * (4 * c + 2 * t + j), 16 * (4 * c + 2 * t + j) + 16)
-                        cols = slice(128 * (2 * c + j), 128 * (2 * c + j) + 128)
-                        for i in range(12):
-                            eh[16 * i : 16 * i + 16, cols] = dh[rows, 128 * i : 128 * i + 128]
-                            el[16 * i : 16 * i + 16, cols] = dl[rows, 128 * i : 128 * i + 128]
-                along = right(eh[...], el[...], xth[...], xtl[...])
-                uh, ul = split(along)
-                lanes = slice(128 * t, 128 * t + 128)
-                for c in range(2):
-                    q[192 * c : 192 * c + 192, lanes] = uh[:, 128 * c : 128 * c + 128]
-                    q[384 + 192 * c : 576 + 192 * c, lanes] = ul[:, 128 * c : 128 * c + 128]
-
-        def body(k, carry):
-            pair = lax.rem(me // 2 + k, 8)
-            lanes = pl.ds(pl.multiple_of(pair * 256, 256), 256)
-            place = onehot[:, lanes]
-            keep = mask[:, lanes]
-            both = dot(q[...], place)
-            found = both[0:384] + both[384:768]
-            picked = jnp.sum(found.reshape(ROWS, 16, 256) * keep[None], axis=1)
-            send[rnd, 2 * pair] = picked[:, 0:128]
-            send[rnd, 2 * pair + 1] = picked[:, 128:256]
-
-            @pl.when(k > 0)
-            def _():
-                post(rnd, lax.rem(me // 2 + k + 7, 8))
-
-            return carry
+                    lanes = slice(128 * t, 128 * t + 128)
+                    cols = slice(128 * c, 128 * c + 128)
+                    q[96 * c : 96 * c + 96, lanes] = uh[96 * t : 96 * t + 96, cols]
+                    q[192 + 96 * c : 288 + 96 * c, lanes] = ul[96 * t : 96 * t + 96, cols]
 
         with jax.named_scope("stick_pick"):
-            lax.fori_loop(0, 8, body, 0)
-            post(rnd, lax.rem(me // 2 + 7, 8))
+            for k in range(5):
+                if k < 4:
+                    quad = lax.rem(me // 4 + k, 4)
+                    lanes = pl.ds(pl.multiple_of(quad * 512, 512), 512)
+                    both = dot(q[...], onehot[:, lanes])
+                    found = both[0:192] + both[192:384]
+                    picked = jnp.sum(found.reshape(ROWS, 8, 512) * mask[:, lanes][None], axis=1)
+                    for n in range(4):
+                        send[rnd, 4 * quad + n] = picked[:, 128 * n : 128 * n + 128]
+                if k > 0:
+                    post(rnd, lax.rem(me // 4 + k + 3, 4))
             recv[rnd, me] = send[rnd, me]
 
-    def post(rnd, pair):
-        for half in range(2):
-            owner = 2 * pair + half
+    def post(rnd, quad):
+        for n in range(4):
+            owner = 4 * quad + n
 
             @pl.when(owner != me)
             def _():
@@ -516,6 +511,9 @@
     for o in range(4):
         small_send[0, o : o + 1, 0:16] = projections(o, 16)
     small_exchange(0)
+    with jax.named_scope("unpack"):
+        loads["vloc"].wait()
+        unpack(vloc_flat, vloc)
     found = small_total(0) * (1.0 / (2.0 * GRID * 2048))
     eye = (row[0:16] == lane[0:16]).astype(f32)
     spread(eye, found)
@@ -581,27 +579,28 @@
     small_send[1] = jnp.zeros((8, 128), f32)
     for o in range(4):
         small_send[1, o : o + 1, :] = projections(o, 128)
-    norms = stick_sum(direction, direction)
+    small_send[1, 4:5, :] = packed(stick_sum(direction, direction))
+    small_exchange(1)
     curves = stick_sum(direction, direction, True)
     fill_planes(2, field0)
     local = grid_sum(field0, field0)
-    small_send[1, 4:5, :] = packed(norms)
-    small_send[1, 5:6, :] = packed([curves[b] + local[b] for b in range(2)])
-    small_exchange(1)
+    small_send[3] = jnp.zeros((8, 128), f32)
+    small_send[3, 0:1, :] = packed([curves[b] + local[b] for b in range(2)])
+    small_exchange(3)
     to_sticks(3, vloc, field0)
     sums = small_total(1)
     values0 = sums[0:4]
     coupled0 = coupled_rows(sums)[0:4]
     nonlocal0 = band_dots(values0, coupled0)
     norm0 = unpacked(sums[4:5])
-    curve0 = [c + n for c, n in zip(unpacked(sums[5:6]), nonlocal0)]
-    alpha0 = [norm0[b] / curve0[b] for b in range(2)]
     spread(couple[...], values0)
     for c in range(2):
         for b in range(2):
             at = slice(192 * c + 96 * b, 192 * c + 96 * b + 96)
             vec[1, at, :] = direction[at, :] * (kin[...] + shift[b])
     apply(beta_rows, 128, vec.at[1])
+    curve0 = [c + n for c, n in zip(unpacked(small_total(3)[0:1]), nonlocal0)]
+    alpha0 = [norm0[b] / curve0[b] for b in range(2)]
     arrived(3)
     image[...] += z_forward(3)
     residual = vec.at[1]
@@ -615,16 +614,17 @@
     small_send[2] = jnp.zeros((8, 128), f32)
     for o in range(4):
         small_send[2, o : o + 1, :] = projections(o, 128)
-    norms = stick_sum(residual, residual)
+    small_send[2, 4:5, :] = packed(stick_sum(residual, residual))
+    small_exchange(2)
     selfs = stick_sum(residual, residual, True)
     crosses = stick_sum(residual, direction, True)
     fill_planes(4, field1)
     self_local = grid_sum(field1, field1)
     cross_local = grid_sum(field1, field0)
-    small_send[2, 4:5, :] = packed(norms)
-    small_send[2, 5:6, :] = packed([selfs[b] + self_local[b] for b in range(2)])
-    small_send[2, 6:7, :] = packed([crosses[b] + cross_local[b] for b in range(2)])
-    small_exchange(2)
+    small_send[4] = jnp.zeros((8, 128), f32)
+    small_send[4, 0:1, :] = packed([selfs[b] + self_local[b] for b in range(2)])
+    small_send[4, 1:2, :] = packed([crosses[b] + cross_local[b] for b in range(2)])
+    small_exchange(4)
     with jax.named_scope("products"):
         for p in range(PLANES):
             for b in range(2):
@@ -640,7 +640,9 @@
     self_dots = band_dots(values1, coupled1)
     cross_dots = band_dots(values1, coupled0)
     weight0, weight1 = [], []
-    norm1, self1, cross1 = (unpacked(sums[n : n + 1]) for n in (4, 5, 6))
+    norm1 = unpacked(sums[4:5])
+    sums = small_total(4)
+    self1, cross1 = (unpacked(sums[n : n + 1]) for n in range(2))
     for b in range(2):
         ratio = norm1[b] / norm0[b]
         self_curve = self1[b] + self_dots[b]
@@ -665,29 +667,29 @@
 
     lax.fori_loop(1, nb, part_out, 0)
     part_recv[mb] = part_send[mb]
-    for c in range(2):
-        for b in range(2):
-            at = slice(192 * c + 96 * b, 192 * c + 96 * b + 96)
-            response[c, b] = weight0[b] * direction[at, :] + weight1[b] * residual[at, :]
+    first_out[...] = direction[...]
+    second_out[...] = residual[...]
+    for b in range(2):
+        weights_out[b : b + 1, :] = jnp.broadcast_to(weight0[b], (1, 128))
+        weights_out[2 + b : 3 + b, :] = jnp.broadcast_to(weight1[b], (1, 128))
+    weights_out[4:8, :] = jnp.zeros((4, 128), f32)
 
     def part_in(k, c):
         part_copy(k, 0).wait_recv()
         return c
 
-    with jax.named_scope("part_wait"):
-        lax.fori_loop(1, nb, part_in, 0)
-    cells[0:72, :] = jnp.sum(part_recv[...], axis=0)
-    for y in range(12):
-        density[:, 96 * y : 96 * y + 96] = cells[pl.ds(y, PLANES, stride=12), :][:, 0:96]
-
     def sent(k, c):
         for rnd in range(5):
             ga_copy(rnd, k).wait_send()
-        for rnd in range(3):
+        for rnd in range(5):
             small_copy(rnd, k, None).wait_send()
         return c
 
     lax.fori_loop(1, GROUPS, sent, 0)
+
+    with jax.named_scope("part_wait"):
+        lax.fori_loop(1, nb, part_in, 0)
+    cells_out[...] = jnp.sum(part_recv[...], axis=0)
 
     def band_sent(k, c):
         psi_copy(k, None).wait_send()
@@ -695,6 +697,22 @@
         return c
 
     lax.fori_loop(1, nb, band_sent, 0)
+
+
+OUTS = tuple(
+    pltpu.VMEM(shape, f32) for shape in ((384, 128), (384, 128), (8, 128), (72, 128))
+)
+
+
+def finish(first, second, weights, cells, response, density):
+    for c in range(2):
+        for b in range(2):
+            at = slice(192 * c + 96 * b, 192 * c + 96 * b + 96)
+            response[c, b] = (
+                weights[b : b + 1, :] * first[at, :] + weights[2 + b : 3 + b, :] * second[at, :]
+            )
+    for y in range(12):
+        density[:, 96 * y : 96 * y + 96] = cells[pl.ds(y, PLANES, stride=12), :][:, 0:96]
 
 
 def per_device(psi, vloc, dv, beta, dij, atom_type, stick_xy, band_shift):
@@ -703,15 +721,15 @@
     dma = pltpu.SemaphoreType.DMA
     every = tables(2)
     early, late = every[:2], every[2:]
-    response, density = pl.pallas_call(
+    pieces = pl.pallas_call(
         kernel,
-        out_shape=(
-            jax.ShapeDtypeStruct((2, 2, GRID, 128), f32),
-            jax.ShapeDtypeStruct((PLANES, 12 * GRID), f32),
-        ),
-        in_specs=[smem] * 3 + [vmem] * 4 + [pl.BlockSpec(memory_space=pl.ANY)] * 12,
-        out_specs=(vmem, vmem),
+        out_shape=OUTS,
+        in_specs=[smem] * 3 + [pl.BlockSpec(memory_space=pl.ANY)] * 16,
+        out_specs=(vmem,) * 4,
         scratch_shapes=[
+            pltpu.VMEM((2, 2, GRID, 128), bf16),
+            pltpu.VMEM((GROUPS, 128), jnp.int32),
+            *[pltpu.VMEM(t.shape, t.dtype) for t in early],
             pltpu.VMEM((PLANES, GRID * GRID), f32),
             pltpu.VMEM((PLANES, GRID * GRID), f32),
             *[pltpu.VMEM(t.shape, t.dtype) for t in late],
@@ -720,24 +738,25 @@
             pltpu.VMEM((GRID, 768), f32),
             pltpu.VMEM((768, 128), f32),
             pltpu.VMEM((8, 2, 2, GRID, 128), bf16),
-            pltpu.VMEM((256, 2048), bf16),
-            pltpu.VMEM((16, 2048), f32),
+            pltpu.VMEM((512, 2048), bf16),
+            pltpu.VMEM((8, 2048), f32),
             pltpu.VMEM((5, GROUPS, ROWS, 128), f32),
             pltpu.VMEM((5, GROUPS, ROWS, 128), f32),
-            pltpu.VMEM((3, 8, 128), f32),
-            pltpu.VMEM((3, GROUPS, 8, 128), f32),
+            pltpu.VMEM((5, 8, 128), f32),
+            pltpu.VMEM((5, GROUPS, 8, 128), f32),
             pltpu.VMEM((8, 72, 128), f32),
             pltpu.VMEM((8, 72, 128), f32),
-            pltpu.VMEM((768, 2048), bf16),
-            pltpu.VMEM((384, 256), f32),
-            pltpu.VMEM((192, 512), bf16),
-            pltpu.VMEM((192, 512), bf16),
+            pltpu.VMEM((384, 2048), bf16),
+            pltpu.VMEM((192, 512), f32),
+            pltpu.VMEM((384, 512), f32),
+            pltpu.VMEM((384, 512), bf16),
+            pltpu.VMEM((384, 512), bf16),
             pltpu.VMEM((128, 1536), bf16),
             pltpu.VMEM((128, 1536), bf16),
             pltpu.VMEM((192, 1536), f32),
             pltpu.VMEM((192, 1536), f32),
             pltpu.VMEM((192, 1536), f32),
-            pltpu.VMEM((768, 256), bf16),
+            pltpu.VMEM((384, 512), bf16),
             pltpu.VMEM((4, 128, 128), f32),
             pltpu.VMEM((4, 128, 128), f32),
             pltpu.VMEM((128, 128), f32),
@@ -746,13 +765,13 @@
             pltpu.VMEM((GRID, 128), f32),
             pltpu.VMEM((8, 2048), f32),
             pltpu.VMEM((192, 1536), f32),
-            dma((12,)),
+            dma((16,)),
             dma((8,)),
             dma((8,)),
             dma((5, GROUPS)),
             dma((5, GROUPS)),
-            dma((3, GROUPS)),
-            dma((3, GROUPS)),
+            dma((5, GROUPS)),
+            dma((5, GROUPS)),
             dma((8,)),
             dma((8,)),
         ],
@@ -763,7 +782,15 @@
         band_shift, dij, atom_type, psi, stick_xy.reshape(GROUPS, 128), *early,
         vloc, dv, *late, beta,
     )
-    return response, density
+    return pl.pallas_call(
+        finish,
+        out_shape=(
+            jax.ShapeDtypeStruct((2, 2, GRID, 128), f32),
+            jax.ShapeDtypeStruct((PLANES, 12 * GRID), f32),
+        ),
+        in_specs=[vmem] * 4,
+        out_specs=(vmem, vmem),
+    )(*(pltpu.with_memory_space_constraint(p, pltpu.VMEM) for p in pieces))
 
 
 def solution(mesh):

time: 81 us -> 72.2 us (0.89)
  Pallas kernels: 77.1 us -> 71.4 us
  local copies, waits for them, and re-layouts: 3 us -> 0 us
    pallas_call x1 -> x2, Pallas kernels: 77.1 us -> 71.4 us  [the longest x1 70.7 us: per_device(): pl.pallas_call(kernel, out_shape=OUTS, in_specs=[smem] * 3 + [pl.BlockSpe...]
    unnamed x2 -> x0, local copies, waits for them, and re-layouts: 3 us -> none
where the time goes in v2:
time: 72.2 us; the launch traced here: 72 us
  Pallas kernels  71.4 us (99%)
    pallas_call x1, Pallas kernels, per_device(): pl.pallas_call(kernel, out_shape=OUTS, in_specs=[smem] * 3 + [pl.BlockSpe...  70.7 us

profile of v2, /device:TPU:1, one launch (start us, length us, event | category | flops | bytes accessed | tf_op | source)
XLA Modules:
  0.0 72.0 jit_solution(15608684720194204824)
XLA Ops:
  0.6 70.7 %shard_map.194 = (f32[384,128]{1,0:T(8,128)S(1)}, f32[384,128]{1,0:T(8,128)S(1)}, f32[8,128]{1,0:T(8,128)S(1)}, f32[72,128]{1,0:T(8,128)S(1)}) custom-call(f32[2]{0:T(128)} %shift.1, f32[2,4,4]{2,1,0:T(4,128)} %dij.1, s32[32]{0:T(128)} %kind.1, bf16[2,2,96,128]{3,2,1,0:T(8,128)(2,1)} %psi_hbm.1, s32[16,128]{1,0:T(8,128)} %bitcast.1, ...), custom_call_target="tpu_custom_call" | custom-call | tf_op jit(solution)/shard_map/pallas_call | solution.py:724
  71.3 0.7 shard_map.195

commit v3 on v2

--- a/solution.py
+++ b/solution.py
@@ -30,14 +30,16 @@
     return high, low
 
 
-def tables(bands):
+def tables():
     unit = 2.0 * math.pi / GRID
     cells = np.arange(GRID)
     freqs = np.arange(SIDE) - SIDE // 2
     along_z = complex_table(unit * (cells[:, None] * cells[None, :] % GRID))
     along_z = along_z.reshape(2, 2, GROUPS, PLANES, GRID)
-    z_table = np.einsum("oidpk,be->dopbiek", along_z, np.eye(bands))
-    z_table = z_table.reshape(GROUPS * 2 * PLANES * bands, 2 * bands * GRID)
+    z_table = np.einsum("oidpk->dopik", along_z).reshape(GROUPS, 12, 2 * GRID)
+    z_table = np.concatenate(
+        [z_table[:, :8].reshape(128, -1), z_table[:, 8:].reshape(64, -1)], axis=0
+    )
     along_x = np.zeros((2, 2, SIDE, 128))
     along_x[..., :GRID] = complex_table(unit * (freqs[:, None] * cells[None, :] % GRID))
     x_table = np.einsum("oikx,be->ibkoex", along_x, np.eye(2)).reshape(256, 512)
@@ -45,7 +47,10 @@
     along_y = along_y.reshape(2, 2, GRID, 8, 8)
     y_table = np.einsum("oiygl->oyilg", along_y).reshape(192, 128)
     out = []
-    for table in (z_table, z_table.T, x_table, x_table.T, y_table):
+    for table in (z_table, z_table.T):
+        high, low = halves(np.ascontiguousarray(table))
+        out.append(np.concatenate([high, low, high], axis=1))
+    for table in (x_table, x_table.T, y_table):
         out.extend(halves(np.ascontiguousarray(table)))
     high, low = halves(np.ascontiguousarray(y_table.T))
     out.append(np.concatenate([high, high, low], axis=1))
@@ -65,11 +70,9 @@
     return high, (x - high.astype(f32)).astype(bf16)
 
 
-def left(high, low, x):
+def deep(table, x):
     xh, xl = split(x)
-    return dot(
-        jnp.concatenate([high, high, low], axis=1), jnp.concatenate([xh, xl, xh], axis=0)
-    )
+    return dot(table, jnp.concatenate([xh, xh, xl], axis=0))
 
 
 def right(ah, al, high, low):
@@ -87,14 +90,14 @@
 
 
 def kernel(
-    shift, dij, kind, psi_hbm, sticks_hbm, zh_hbm, zl_hbm, vloc_hbm, dv_hbm, zth_hbm, ztl_hbm, xh_hbm, xl_hbm, xth_hbm, xtl_hbm,
+    shift, dij, kind, psi_hbm, sticks_hbm, z3_hbm, vloc_hbm, dv_hbm, zt3_hbm, xh_hbm, xl_hbm, xth_hbm, xtl_hbm,
     yh_hbm, yl_hbm, yt3_hbm, beta_hbm,
     first_out, second_out, weights_out, cells_out,
-    psi, sticks, zh, zl, vloc_flat, dv_flat, zth, ztl, xh, xl, xth, xtl, yh, yl, yt3,
+    psi, sticks, z3, vloc_flat, dv_flat, zt3, xh, xl, xth, xtl, yh, yl, yt3,
     beta, vloc, dv, cells, occupied, onehot, mask, send, recv, small_send, small_recv,
     part_send, part_recv, lhs, grid, ex, eh, el, dh, dl, psi_field, field0, field1,
     q, proj, coef, couple, vec, image, kin, own, dens,
-    load_sem, psi_ssem, psi_rsem, ssem, rsem, tssem, trsem, dssem, drsem,
+    load_sem, psi_sem, ssem, rsem, rall, tssem, trsem, part_sem,
 ):
     me = lax.axis_index("ga")
     mb = lax.axis_index("band")
@@ -118,36 +121,43 @@
     lax.fori_loop(1, nb, greet_band, 0)
     loads = {}
     pairs = dict(
-        psi=(psi_hbm, psi), zh=(zh_hbm, zh), zl=(zl_hbm, zl), sticks=(sticks_hbm, sticks),
+        psi=(psi_hbm, psi), z3=(z3_hbm, z3), sticks=(sticks_hbm, sticks),
         dv=(dv_hbm, dv_flat), xh=(xh_hbm, xh), xl=(xl_hbm, xl), yh=(yh_hbm, yh),
         yl=(yl_hbm, yl), yt3=(yt3_hbm, yt3), xth=(xth_hbm, xth), xtl=(xtl_hbm, xtl),
-        zth=(zth_hbm, zth), ztl=(ztl_hbm, ztl), vloc=(vloc_hbm, vloc_flat),
+        zt3=(zt3_hbm, zt3), vloc=(vloc_hbm, vloc_flat),
         beta=(beta_hbm, beta),
     )
     for at, (name, (source, target)) in enumerate(pairs.items()):
         loads[name] = pltpu.make_async_copy(source, target, load_sem.at[at])
         loads[name].start()
 
+    def came(rnd, owner):
+        return rsem.at[rnd // 2, owner] if rnd % 2 == 0 else rall.at[rnd // 2]
+
+    def copy(source, target, gone, landed, where):
+        return pltpu.make_async_remote_copy(
+            src_ref=source, dst_ref=target, send_sem=gone, recv_sem=landed,
+            device_id=where, device_id_type=MESH,
+        )
+
     def ga_copy(rnd, k):
         other = lax.rem(me + k, GROUPS)
-        return pltpu.make_async_remote_copy(
-            src_ref=send.at[rnd, other],
-            dst_ref=recv.at[rnd, me],
-            send_sem=ssem.at[rnd, other],
-            recv_sem=rsem.at[rnd, me],
-            device_id=(other, mb),
-            device_id_type=MESH,
+        return copy(
+            send.at[rnd, other], recv.at[rnd, me], ssem.at[rnd], came(rnd, me), (other, mb)
         )
 
     def ga_landed(rnd, k):
         other = lax.rem(me + k, GROUPS)
-        return pltpu.make_async_remote_copy(
-            src_ref=send.at[rnd, other],
-            dst_ref=recv.at[rnd, other],
-            send_sem=ssem.at[rnd, other],
-            recv_sem=rsem.at[rnd, other],
-            device_id=(other, mb),
-            device_id_type=MESH,
+        return copy(
+            send.at[rnd, other], recv.at[rnd, other], ssem.at[rnd], came(rnd, other), (other, mb)
+        )
+
+    others = pl.ds(0, GROUPS - 1)
+    right_of = (lax.rem(me + 1, GROUPS), mb)
+
+    def ga_all(rnd):
+        return copy(
+            send.at[rnd, others], recv.at[rnd, others], ssem.at[rnd], came(rnd, 0), right_of
         )
 
     def exchange(rnd):
@@ -160,70 +170,81 @@
 
     @jax.named_scope("arrived")
     def arrived(rnd):
-        def body(k, c):
-            ga_landed(rnd, k).wait_recv()
-            return c
-
-        lax.fori_loop(1, GROUPS, body, 0)
-
-    def small_copy(rnd, k, slot):
-        other = lax.rem(me + k, GROUPS)
-        return pltpu.make_async_remote_copy(
-            src_ref=small_send.at[rnd],
-            dst_ref=small_recv.at[rnd, me if slot is None else other],
-            send_sem=tssem.at[rnd, other],
-            recv_sem=trsem.at[rnd, me if slot is None else other],
-            device_id=(other, mb),
-            device_id_type=MESH,
-        )
+        ga_all(rnd).wait_recv()
 
     def small_exchange(rnd):
         def body(k, c):
-            small_copy(rnd, k, None).start()
+            copy(
+                small_send.at[rnd], small_recv.at[rnd, me], tssem.at[rnd], trsem.at[rnd],
+                (lax.rem(me + k, GROUPS), mb),
+            ).start()
             return c
 
         lax.fori_loop(1, GROUPS, body, 0)
         small_recv[rnd, me] = small_send[rnd]
 
+    def small_all(rnd):
+        landed = small_recv.at[rnd, others]
+        return copy(landed, landed, tssem.at[rnd], trsem.at[rnd], right_of)
+
     def small_total(rnd):
-        def body(k, c):
-            small_copy(rnd, k, 0).wait_recv()
-            return c
-
         with jax.named_scope("small_wait"):
-            lax.fori_loop(1, GROUPS, body, 0)
+            small_all(rnd).wait_recv()
         return jnp.sum(small_recv[rnd], axis=0)
 
-    def psi_copy(k, slot):
+    def psi_copy(k):
+        where = (me, lax.rem(mb + k, nb))
+        return copy(psi, occupied.at[mb], psi_sem.at[0], psi_sem.at[1], where)
+
+    rest = pl.ds(0, nb - 1)
+    after = (me, lax.rem(mb + 1, nb))
+
+    def psi_all():
+        return copy(occupied.at[rest], occupied.at[rest], psi_sem.at[0], psi_sem.at[1], after)
+
+    def part_copy(k):
         other = lax.rem(mb + k, nb)
-        return pltpu.make_async_remote_copy(
-            src_ref=psi,
-            dst_ref=occupied.at[mb if slot is None else other],
-            send_sem=psi_ssem.at[other],
-            recv_sem=psi_rsem.at[mb if slot is None else other],
-            device_id=(me, other),
-            device_id_type=MESH,
-        )
-
-    def part_copy(k, slot):
-        other = lax.rem(mb + k, nb)
-        return pltpu.make_async_remote_copy(
-            src_ref=part_send.at[other],
-            dst_ref=part_recv.at[mb if slot is None else other],
-            send_sem=dssem.at[other],
-            recv_sem=drsem.at[mb if slot is None else other],
-            device_id=(me, other),
-            device_id_type=MESH,
-        )
-
-    for name in ("psi", "zh", "zl"):
+        return copy(
+            part_send.at[other], part_recv.at[mb], part_sem.at[0], part_sem.at[1], (me, other)
+        )
+
+    def part_all():
+        return copy(part_send.at[rest], part_recv.at[rest], part_sem.at[0], part_sem.at[1], after)
+
+    def dealt(rnd, planes):
+        for d in range(GROUPS):
+            head = planes[8 * d : 8 * d + 8]
+            tail = planes[128 + 4 * d : 132 + 4 * d]
+            send[rnd, d, 0:8] = head[:, 0:128]
+            send[rnd, d, 8:16] = jnp.concatenate([tail[:, 0:128], tail[:, 128:256]], axis=0)
+            send[rnd, d, 16:24] = head[:, 128:256]
+
+    def collected(rnd):
+        rows = [
+            jnp.concatenate([recv[rnd, d, 0:8], recv[rnd, d, 16:24]], axis=1)
+            for d in range(GROUPS)
+        ]
+        for d in range(0, GROUPS, 2):
+            even, odd = recv[rnd, d, 8:16], recv[rnd, d + 1, 8:16]
+            rows.append(
+                jnp.concatenate(
+                    [
+                        jnp.concatenate([even[0:4], odd[0:4]], axis=0),
+                        jnp.concatenate([even[4:8], odd[4:8]], axis=0),
+                    ],
+                    axis=1,
+                )
+            )
+        return jnp.concatenate(rows, axis=0)
+
+    for name in ("psi", "z3"):
         loads[name].wait()
     with jax.named_scope("z_psi"):
-        wide = psi[...].reshape(384, 128)
-        send[0] = dot(
-            jnp.concatenate([zh[...], zl[...]], axis=1),
-            jnp.concatenate([wide, wide], axis=0),
-        ).reshape(GROUPS, ROWS, 128)
+        wide = jnp.concatenate(
+            [jnp.concatenate([psi[c, 0], psi[c, 1]], axis=1) for c in range(2)], axis=0
+        )
+        dealt(0, dot(z3[:, 0:384], jnp.concatenate([wide, wide], axis=0)))
+
     def places(xy):
         flat = xy.astype(f32)
         y = jnp.floor((flat + 0.5) * (1.0 / GRID))
@@ -299,7 +320,7 @@
     exchange(0)
 
     def psi_out(k, c):
-        psi_copy(k, None).start()
+        psi_copy(k).start()
         return c
 
     lax.fori_loop(1, nb, psi_out, 0)
@@ -308,7 +329,7 @@
     with jax.named_scope("unpack"):
         loads["dv"].wait()
         unpack(dv_flat, dv)
-    for name in ("xh", "xl", "yh", "yl", "yt3", "xth", "xtl", "zth", "ztl"):
+    for name in ("xh", "xl", "yh", "yl", "yt3", "xth", "xtl", "zt3"):
         loads[name].wait()
     ones = jnp.ones((256, 128), bf16)
 
@@ -327,9 +348,10 @@
             cols = pl.ds(pl.multiple_of(src * 128, 128), 128)
             keep = mask[:, cols]
             for n, part in enumerate((upper, lower)):
-                for r in range(0, ROWS, 2):
-                    two = [jnp.broadcast_to(part[r + e : r + e + 1], (8, 128)) * keep for e in (0, 1)]
-                    at = 192 * n + 8 * r
+                for index in range(12):
+                    pair = (index, index + 16 if index < 8 else index + 4)
+                    two = [jnp.broadcast_to(part[r : r + 1], (8, 128)) * keep for r in pair]
+                    at = 192 * n + 16 * index
                     lhs[at : at + 16, cols] = jnp.concatenate(two, axis=0).astype(bf16)
             return c
 
@@ -386,13 +408,21 @@
                             el[at : at + 16, cols] = ul
         with jax.named_scope("stick_x"):
             along = right(eh[...], el[...], xth[...], xtl[...])
-            uh, ul = split(along)
-            for t in range(4):
-                for c in range(2):
+            for r in range(0, ROWS, 2):
+                if r < 12:
+                    index, b = r, 0
+                else:
+                    index, b = (r - 4, 1) if r < 16 else (r - 16, 1)
+                for t in range(4):
+                    two = []
+                    for n in (index, index + 1):
+                        at = 96 * t + 8 * (2 * (n % PLANES) + b)
+                        col = 128 * (n // PLANES)
+                        two.append(along[at : at + 8, col : col + 128])
+                    uh, ul = split(jnp.concatenate(two, axis=0))
                     lanes = slice(128 * t, 128 * t + 128)
-                    cols = slice(128 * c, 128 * c + 128)
-                    q[96 * c : 96 * c + 96, lanes] = uh[96 * t : 96 * t + 96, cols]
-                    q[192 + 96 * c : 288 + 96 * c, lanes] = ul[96 * t : 96 * t + 96, cols]
+                    q[8 * r : 8 * r + 16, lanes] = uh
+                    q[192 + 8 * r : 208 + 8 * r, lanes] = ul
 
         with jax.named_scope("stick_pick"):
             for k in range(5):
@@ -417,7 +447,7 @@
                 ga_copy(rnd, owner - me + GROUPS).start()
 
     def z_forward(rnd):
-        return left(zth[...], ztl[...], recv[rnd].reshape(384, 128))
+        return deep(zt3[...], collected(rnd))
 
     def project(load, count, source):
         step = 4
@@ -425,7 +455,11 @@
         def body(g, c):
             sums = [[None] * 4 for _ in range(step)]
             for z in range(GRID // 8):
-                v = [source[96 * n + 8 * z : 96 * n + 8 * z + 8, :] for n in range(4)]
+                v = [
+                    source[96 * c + 8 * z : 96 * c + 8 * z + 8, 128 * b : 128 * b + 128]
+                    for c in range(2)
+                    for b in range(2)
+                ]
                 for t in range(step):
                     p0, p1 = load(g * step + t, 8 * z, 8)
                     for b in range(2):
@@ -474,7 +508,7 @@
                 return tuple(acc)
 
             init = tuple(
-                base[192 * c + 96 * b + z * rows : 192 * c + 96 * b + z * rows + rows, :]
+                base[96 * c + z * rows : 96 * c + z * rows + rows, 128 * b : 128 * b + 128]
                 for b in range(2)
                 for c in range(2)
             )
@@ -482,8 +516,8 @@
                 done = lax.fori_loop(0, count // 4, body, init)
             for b in range(2):
                 for c in range(2):
-                    at = 192 * c + 96 * b + z * rows
-                    image[at : at + rows, :] = done[2 * b + c]
+                    at = 96 * c + z * rows
+                    image[at : at + rows, 128 * b : 128 * b + 128] = done[2 * b + c]
 
     def beta_rows(j, at=0, rows=GRID):
         return beta[0, j, at : at + rows, :], beta[1, j, at : at + rows, :]
@@ -498,13 +532,9 @@
     fill_planes(0, psi_field)
     to_sticks(1, dv, psi_field)
 
-    def psi_in(k, c):
-        psi_copy(k, 0).wait_recv()
-        return c
-
     arrived(1)
     vec[1] = z_forward(1)
-    lax.fori_loop(1, nb, psi_in, 0)
+    psi_all().wait_recv()
 
     project(psi_rows, 16, vec.at[1])
     small_send[0] = jnp.zeros((8, 128), f32)
@@ -522,15 +552,14 @@
     vec[0] = image[...]
 
     def transform_out(rnd, source):
-        send[rnd] = left(zh[...], zl[...], source[...]).reshape(GROUPS, ROWS, 128)
+        dealt(rnd, deep(z3[...], source[...]))
         exchange(rnd)
 
     def stick_sum(a, b, weight=None):
         out = []
         for n in range(2):
-            s0 = slice(96 * n, 96 * n + 96)
-            s1 = slice(192 + 96 * n, 288 + 96 * n)
-            both = a[s0, :] * b[s0, :] + a[s1, :] * b[s1, :]
+            at = slice(128 * n, 128 * n + 128)
+            both = a[0:96, at] * b[0:96, at] + a[96:192, at] * b[96:192, at]
             if weight is not None:
                 both = both * (kin[...] + shift[n])
             out.append(row_sum(both))
@@ -596,8 +625,8 @@
     spread(couple[...], values0)
     for c in range(2):
         for b in range(2):
-            at = slice(192 * c + 96 * b, 192 * c + 96 * b + 96)
-            vec[1, at, :] = direction[at, :] * (kin[...] + shift[b])
+            at, of = slice(96 * c, 96 * c + 96), slice(128 * b, 128 * b + 128)
+            vec[1, at, of] = direction[at, of] * (kin[...] + shift[b])
     apply(beta_rows, 128, vec.at[1])
     curve0 = [c + n for c, n in zip(unpacked(small_total(3)[0:1]), nonlocal0)]
     alpha0 = [norm0[b] / curve0[b] for b in range(2)]
@@ -606,8 +635,8 @@
     residual = vec.at[1]
     for c in range(2):
         for b in range(2):
-            at = slice(192 * c + 96 * b, 192 * c + 96 * b + 96)
-            residual[at, :] = direction[at, :] - alpha0[b] * image[at, :]
+            at, of = slice(96 * c, 96 * c + 96), slice(128 * b, 128 * b + 128)
+            residual[at, of] = direction[at, of] - alpha0[b] * image[at, of]
 
     transform_out(4, residual)
     project(beta_rows, 128, residual)
@@ -662,7 +691,7 @@
                 part_send[i, 12 * p : 12 * p + 12, :] = total[12 * i : 12 * i + 12, :]
 
     def part_out(k, c):
-        part_copy(k, None).start()
+        part_copy(k).start()
         return c
 
     lax.fori_loop(1, nb, part_out, 0)
@@ -674,42 +703,28 @@
         weights_out[2 + b : 3 + b, :] = jnp.broadcast_to(weight1[b], (1, 128))
     weights_out[4:8, :] = jnp.zeros((4, 128), f32)
 
-    def part_in(k, c):
-        part_copy(k, 0).wait_recv()
-        return c
-
-    def sent(k, c):
-        for rnd in range(5):
-            ga_copy(rnd, k).wait_send()
-        for rnd in range(5):
-            small_copy(rnd, k, None).wait_send()
-        return c
-
-    lax.fori_loop(1, GROUPS, sent, 0)
-
+    for rnd in range(5):
+        ga_all(rnd).wait_send()
+        small_all(rnd).wait_send()
+    psi_all().wait_send()
     with jax.named_scope("part_wait"):
-        lax.fori_loop(1, nb, part_in, 0)
+        part_all().wait_recv()
     cells_out[...] = jnp.sum(part_recv[...], axis=0)
 
-    def band_sent(k, c):
-        psi_copy(k, None).wait_send()
-        part_copy(k, None).wait_send()
-        return c
-
-    lax.fori_loop(1, nb, band_sent, 0)
+    part_all().wait_send()
 
 
 OUTS = tuple(
-    pltpu.VMEM(shape, f32) for shape in ((384, 128), (384, 128), (8, 128), (72, 128))
+    pltpu.VMEM(shape, f32) for shape in ((192, 256), (192, 256), (8, 128), (72, 128))
 )
 
 
 def finish(first, second, weights, cells, response, density):
     for c in range(2):
         for b in range(2):
-            at = slice(192 * c + 96 * b, 192 * c + 96 * b + 96)
+            at, of = slice(96 * c, 96 * c + 96), slice(128 * b, 128 * b + 128)
             response[c, b] = (
-                weights[b : b + 1, :] * first[at, :] + weights[2 + b : 3 + b, :] * second[at, :]
+                weights[b : b + 1, :] * first[at, of] + weights[2 + b : 3 + b, :] * second[at, of]
             )
     for y in range(12):
         density[:, 96 * y : 96 * y + 96] = cells[pl.ds(y, PLANES, stride=12), :][:, 0:96]
@@ -719,12 +734,12 @@
     vmem = pl.BlockSpec(memory_space=pltpu.VMEM)
     smem = pl.BlockSpec(memory_space=pltpu.SMEM)
     dma = pltpu.SemaphoreType.DMA
-    every = tables(2)
-    early, late = every[:2], every[2:]
+    every = tables()
+    early, late = every[:1], every[1:]
     pieces = pl.pallas_call(
         kernel,
         out_shape=OUTS,
-        in_specs=[smem] * 3 + [pl.BlockSpec(memory_space=pl.ANY)] * 16,
+        in_specs=[smem] * 3 + [pl.BlockSpec(memory_space=pl.ANY)] * 14,
         out_specs=(vmem,) * 4,
         scratch_shapes=[
             pltpu.VMEM((2, 2, GRID, 128), bf16),
@@ -760,20 +775,19 @@
             pltpu.VMEM((4, 128, 128), f32),
             pltpu.VMEM((4, 128, 128), f32),
             pltpu.VMEM((128, 128), f32),
-            pltpu.VMEM((2, 384, 128), f32),
-            pltpu.VMEM((384, 128), f32),
+            pltpu.VMEM((2, 192, 256), f32),
+            pltpu.VMEM((192, 256), f32),
             pltpu.VMEM((GRID, 128), f32),
             pltpu.VMEM((8, 2048), f32),
             pltpu.VMEM((192, 1536), f32),
             dma((16,)),
-            dma((8,)),
-            dma((8,)),
-            dma((5, GROUPS)),
-            dma((5, GROUPS)),
-            dma((5, GROUPS)),
-            dma((5, GROUPS)),
-            dma((8,)),
-            dma((8,)),
+            dma((2,)),
+            dma((5,)),
+            dma((3, GROUPS)),
+            dma((2,)),
+            dma((5,)),
+            dma((5,)),
+            dma((2,)),
         ],
         compiler_params=pltpu.CompilerParams(
             collective_id=0, has_side_effects=True, vmem_limit_bytes=60 * 1024 * 1024

time: 72.2 us -> 68.7 us (0.952)
  Pallas kernels: 71.4 us -> 68 us
    pallas_call x1, Pallas kernels: 70.7 us -> 67.2 us  [per_device(): pl.pallas_call(kernel, out_shape=OUTS, in_specs=[smem] * 3 + [pl.BlockSpe...]
where the time goes in v3:
time: 68.7 us; the launch traced here: 68.6 us
  Pallas kernels  68 us (99%)
    pallas_call x1, Pallas kernels, per_device(): pl.pallas_call(kernel, out_shape=OUTS, in_specs=[smem] * 3 + [pl.BlockSpe...  67.2 us

profile of v3, /device:TPU:1, one launch (start us, length us, event | category | flops | bytes accessed | tf_op | source)
XLA Modules:
  0.0 68.6 jit_solution(10262528159835037318)
XLA Ops:
  0.6 67.2 %shard_map.176 = (f32[192,256]{1,0:T(8,128)S(1)}, f32[192,256]{1,0:T(8,128)S(1)}, f32[8,128]{1,0:T(8,128)S(1)}, f32[72,128]{1,0:T(8,128)S(1)}) custom-call(f32[2]{0:T(128)} %shift.1, f32[2,4,4]{2,1,0:T(4,128)} %dij.1, s32[32]{0:T(128)} %kind.1, bf16[2,2,96,128]{3,2,1,0:T(8,128)(2,1)} %psi_hbm.1, s32[16,128]{1,0:T(8,128)} %bitcast.1, ...), custom_call_target="tpu_custom_call" | custom-call | tf_op jit(solution)/shard_map/pallas_call | solution.py:739
  67.9 0.7 %shard_map.177 = (f32[2,2,96,128]{3,2,1,0:T(8,128)}, f32[6,1152]{1,0:T(8,128)}) custom-call(f32[192,256]{1,0:T(8,128)S(1)} %get-tuple-element.6.first, f32[192,256]{1,0:T(8,128)S(1)} %get-tuple-element.7.second, f32[8,128]{1,0:T(8,128)S(1)} %get-tuple-element.8.weights, f32[72,128]{1,0:T(8,128)S(1)} %get-tuple-element.9.cells), custom_call_target="tpu_custom_call" | custom-call | tf_op jit(solution)/shard_map/pallas_call | solution.py:799

commit v4 on v3

--- a/solution.py
+++ b/solution.py
@@ -90,10 +90,10 @@
 
 
 def kernel(
-    shift, dij, kind, psi_hbm, sticks_hbm, z3_hbm, vloc_hbm, dv_hbm, zt3_hbm, xh_hbm, xl_hbm, xth_hbm, xtl_hbm,
+    shift_hbm, dij_hbm, kind_hbm, psi_hbm, sticks_hbm, z3_hbm, vloc_hbm, dv_hbm, zt3_hbm, xh_hbm, xl_hbm, xth_hbm, xtl_hbm,
     yh_hbm, yl_hbm, yt3_hbm, beta_hbm,
     first_out, second_out, weights_out, cells_out,
-    psi, sticks, z3, vloc_flat, dv_flat, zt3, xh, xl, xth, xtl, yh, yl, yt3,
+    shift, dij, kind, psi, sticks, z3, vloc_flat, dv_flat, zt3, xh, xl, xth, xtl, yh, yl, yt3,
     beta, vloc, dv, cells, occupied, onehot, mask, send, recv, small_send, small_recv,
     part_send, part_recv, lhs, grid, ex, eh, el, dh, dl, psi_field, field0, field1,
     q, proj, coef, couple, vec, image, kin, own, dens,
@@ -102,26 +102,30 @@
     me = lax.axis_index("ga")
     mb = lax.axis_index("band")
     nb = 8
+    mx, my = me // 4, lax.rem(me, 4)
+
+    def peer(dx, dy):
+        return lax.rem(mx + dx, 4) * 4 + lax.rem(my + dy, 4)
+
+    OFFSETS = sorted(
+        ((dx, dy) for dx in range(4) for dy in range(4) if dx or dy),
+        key=lambda o: -(min(o[0], 4 - o[0]) + min(o[1], 4 - o[1])),
+    )
+    X_ORDER = (2, 1, 3, 0)
+    BANDS_FAR = (4, 5, 3, 2, 6, 7, 1)
 
     barrier = pltpu.get_barrier_semaphore()
 
-    def greet_ga(k, c):
-        pl.semaphore_signal(
-            barrier, inc=1, device_id=(lax.rem(me + k, GROUPS), mb), device_id_type=MESH
-        )
-        return c
-
-    def greet_band(k, c):
+    for offset in OFFSETS:
+        pl.semaphore_signal(barrier, inc=1, device_id=(peer(*offset), mb), device_id_type=MESH)
+    for k in BANDS_FAR:
         pl.semaphore_signal(
             barrier, inc=1, device_id=(me, lax.rem(mb + k, nb)), device_id_type=MESH
         )
-        return c
-
-    lax.fori_loop(1, GROUPS, greet_ga, 0)
-    lax.fori_loop(1, nb, greet_band, 0)
     loads = {}
     pairs = dict(
         psi=(psi_hbm, psi), z3=(z3_hbm, z3), sticks=(sticks_hbm, sticks),
+        kind=(kind_hbm, kind), dij=(dij_hbm, dij), shift=(shift_hbm, shift),
         dv=(dv_hbm, dv_flat), xh=(xh_hbm, xh), xl=(xl_hbm, xl), yh=(yh_hbm, yh),
         yl=(yl_hbm, yl), yt3=(yt3_hbm, yt3), xth=(xth_hbm, xth), xtl=(xtl_hbm, xtl),
         zt3=(zt3_hbm, zt3), vloc=(vloc_hbm, vloc_flat),
@@ -132,7 +136,7 @@
         loads[name].start()
 
     def came(rnd, owner):
-        return rsem.at[rnd // 2, owner] if rnd % 2 == 0 else rall.at[rnd // 2]
+        return rsem.at[owner] if rnd == 0 else rall.at[rnd - 1]
 
     def copy(source, target, gone, landed, where):
         return pltpu.make_async_remote_copy(
@@ -140,14 +144,12 @@
             device_id=where, device_id_type=MESH,
         )
 
-    def ga_copy(rnd, k):
-        other = lax.rem(me + k, GROUPS)
+    def ga_copy(rnd, other):
         return copy(
             send.at[rnd, other], recv.at[rnd, me], ssem.at[rnd], came(rnd, me), (other, mb)
         )
 
-    def ga_landed(rnd, k):
-        other = lax.rem(me + k, GROUPS)
+    def ga_landed(rnd, other):
         return copy(
             send.at[rnd, other], recv.at[rnd, other], ssem.at[rnd], came(rnd, other), (other, mb)
         )
@@ -161,11 +163,8 @@
         )
 
     def exchange(rnd):
-        def body(k, c):
-            ga_copy(rnd, k).start()
-            return c
-
-        lax.fori_loop(1, GROUPS, body, 0)
+        for offset in OFFSETS:
+            ga_copy(rnd, peer(*offset)).start()
         recv[rnd, me] = send[rnd, me]
 
     @jax.named_scope("arrived")
@@ -173,14 +172,11 @@
         ga_all(rnd).wait_recv()
 
     def small_exchange(rnd):
-        def body(k, c):
+        for offset in OFFSETS:
             copy(
                 small_send.at[rnd], small_recv.at[rnd, me], tssem.at[rnd], trsem.at[rnd],
-                (lax.rem(me + k, GROUPS), mb),
+                (peer(*offset), mb),
             ).start()
-            return c
-
-        lax.fori_loop(1, GROUPS, body, 0)
         small_recv[rnd, me] = small_send[rnd]
 
     def small_all(rnd):
@@ -313,17 +309,16 @@
         for p in range(PLANES):
             out[:, 128 * p : 128 * p + 128] = cells[pl.ds(p, GRID, stride=8), :]
 
+    for name in ("kind", "dij", "shift"):
+        loads[name].wait()
     with jax.named_scope("couple"):
         couple_all()
     with jax.named_scope("barrier"):
         pl.semaphore_wait(barrier, GROUPS - 1 + nb - 1)
     exchange(0)
 
-    def psi_out(k, c):
+    for k in BANDS_FAR:
         psi_copy(k).start()
-        return c
-
-    lax.fori_loop(1, nb, psi_out, 0)
     occupied[mb] = psi[...]
 
     with jax.named_scope("unpack"):
@@ -335,17 +330,11 @@
 
     def fill_planes(rnd, out):
 
-        def body(k, c):
-            src = lax.rem(me + k, GROUPS)
-
-            @pl.when(k > 0)
-            def _():
-                ga_landed(rnd, k).wait_recv()
-
+        def laid(src):
             piece = recv[rnd, src]
             upper = piece.astype(bf16).astype(f32)
             lower = piece - upper
-            cols = pl.ds(pl.multiple_of(src * 128, 128), 128)
+            cols = pl.ds(pl.multiple_of(src * 128, 128) if rnd == 0 else src * 128, 128)
             keep = mask[:, cols]
             for n, part in enumerate((upper, lower)):
                 for index in range(12):
@@ -353,10 +342,25 @@
                     two = [jnp.broadcast_to(part[r : r + 1], (8, 128)) * keep for r in pair]
                     at = 192 * n + 16 * index
                     lhs[at : at + 16, cols] = jnp.concatenate(two, axis=0).astype(bf16)
+
+        def body(k, c):
+            src = lax.rem(me + k, GROUPS)
+
+            @pl.when(k > 0)
+            def _():
+                ga_landed(rnd, src).wait_recv()
+
+            laid(src)
             return c
 
         with jax.named_scope("fill_lhs"):
-            lax.fori_loop(0, GROUPS, body, 0)
+            if rnd == 0:
+                lax.fori_loop(0, GROUPS, body, 0)
+            else:
+                arrived(rnd)
+        if rnd:
+            for src in range(GROUPS):
+                laid(src)
         with jax.named_scope("fill_dot"):
             both = dot_nt(lhs[...], onehot[...])
             grid[...] = both[0:192] + both[192:384]
@@ -425,9 +429,9 @@
                     q[192 + 8 * r : 208 + 8 * r, lanes] = ul
 
         with jax.named_scope("stick_pick"):
-            for k in range(5):
-                if k < 4:
-                    quad = lax.rem(me // 4 + k, 4)
+            for k, dx in enumerate(X_ORDER + (None,)):
+                if dx is not None:
+                    quad = lax.rem(mx + dx, 4)
                     lanes = pl.ds(pl.multiple_of(quad * 512, 512), 512)
                     both = dot(q[...], onehot[:, lanes])
                     found = both[0:192] + both[192:384]
@@ -435,16 +439,10 @@
                     for n in range(4):
                         send[rnd, 4 * quad + n] = picked[:, 128 * n : 128 * n + 128]
                 if k > 0:
-                    post(rnd, lax.rem(me // 4 + k + 3, 4))
+                    for dy in (2, 1, 3, 0):
+                        if X_ORDER[k - 1] or dy:
+                            ga_copy(rnd, peer(X_ORDER[k - 1], dy)).start()
             recv[rnd, me] = send[rnd, me]
-
-    def post(rnd, quad):
-        for n in range(4):
-            owner = 4 * quad + n
-
-            @pl.when(owner != me)
-            def _():
-                ga_copy(rnd, owner - me + GROUPS).start()
 
     def z_forward(rnd):
         return deep(zt3[...], collected(rnd))
@@ -690,11 +688,8 @@
             for i in range(nb):
                 part_send[i, 12 * p : 12 * p + 12, :] = total[12 * i : 12 * i + 12, :]
 
-    def part_out(k, c):
+    for k in BANDS_FAR:
         part_copy(k).start()
-        return c
-
-    lax.fori_loop(1, nb, part_out, 0)
     part_recv[mb] = part_send[mb]
     first_out[...] = direction[...]
     second_out[...] = residual[...]
@@ -732,16 +727,18 @@
 
 def per_device(psi, vloc, dv, beta, dij, atom_type, stick_xy, band_shift):
     vmem = pl.BlockSpec(memory_space=pltpu.VMEM)
-    smem = pl.BlockSpec(memory_space=pltpu.SMEM)
     dma = pltpu.SemaphoreType.DMA
     every = tables()
     early, late = every[:1], every[1:]
     pieces = pl.pallas_call(
         kernel,
         out_shape=OUTS,
-        in_specs=[smem] * 3 + [pl.BlockSpec(memory_space=pl.ANY)] * 14,
+        in_specs=[pl.BlockSpec(memory_space=pl.ANY)] * 17,
         out_specs=(vmem,) * 4,
         scratch_shapes=[
+            pltpu.SMEM((2,), f32),
+            pltpu.SMEM((2, 4, 4), f32),
+            pltpu.SMEM((32,), jnp.int32),
             pltpu.VMEM((2, 2, GRID, 128), bf16),
             pltpu.VMEM((GROUPS, 128), jnp.int32),
             *[pltpu.VMEM(t.shape, t.dtype) for t in early],
@@ -780,11 +777,11 @@
             pltpu.VMEM((GRID, 128), f32),
             pltpu.VMEM((8, 2048), f32),
             pltpu.VMEM((192, 1536), f32),
-            dma((16,)),
+            dma((17,)),
             dma((2,)),
             dma((5,)),
-            dma((3, GROUPS)),
-            dma((2,)),
+            dma((GROUPS,)),
+            dma((4,)),
             dma((5,)),
             dma((5,)),
             dma((2,)),

time: 68.7 us -> 63.2 us (0.920)
  Pallas kernels: 68 us -> 62.4 us
    pallas_call x1, Pallas kernels: 67.2 us -> 61.7 us  [per_device(): pl.pallas_call(kernel, out_shape=OUTS, in_specs=[pl.BlockSpec(memory_spac...]
where the time goes in v4:
time: 63.2 us; the launch traced here: 63.1 us
  Pallas kernels  62.4 us (99%)
  between operations  0.64 us (1%)
    pallas_call x1, Pallas kernels, per_device(): pl.pallas_call(kernel, out_shape=OUTS, in_specs=[pl.BlockSpec(memory_spac...  61.7 us

profile of v4, /device:TPU:1, one launch (start us, length us, event | category | flops | bytes accessed | tf_op | source)
XLA Modules:
  0.0 63.1 jit_solution(10887886668146706118)
XLA Ops:
  0.6 61.7 %shard_map.176 = (f32[192,256]{1,0:T(8,128)S(1)}, f32[192,256]{1,0:T(8,128)S(1)}, f32[8,128]{1,0:T(8,128)S(1)}, f32[72,128]{1,0:T(8,128)S(1)}) custom-call(f32[2]{0:T(128)} %shift_hbm.1, f32[2,4,4]{2,1,0:T(4,128)} %dij_hbm.1, s32[32]{0:T(128)} %kind_hbm.1, bf16[2,2,96,128]{3,2,1,0:T(8,128)(2,1)} %psi_hbm.1, s32[16,128]{1,0:T(8,128)} %bitcast.1, ...), custom_call_target="tpu_custom_call" | custom-call | tf_op jit(solution)/shard_map/pallas_call | solution.py:733
  62.3 0.7 %shard_map.177 = (f32[2,2,96,128]{3,2,1,0:T(8,128)}, f32[6,1152]{1,0:T(8,128)}) custom-call(f32[192,256]{1,0:T(8,128)S(1)} %get-tuple-element.6.first, f32[192,256]{1,0:T(8,128)S(1)} %get-tuple-element.7.second, f32[8,128]{1,0:T(8,128)S(1)} %get-tuple-element.8.weights, f32[72,128]{1,0:T(8,128)S(1)} %get-tuple-element.9.cells), custom_call_target="tpu_custom_call" | custom-call | tf_op jit(solution)/shard_map/pallas_call | solution.py:796

commit v5 on v4

--- a/solution.py
+++ b/solution.py
@@ -54,6 +54,33 @@
         out.extend(halves(np.ascontiguousarray(table)))
     high, low = halves(np.ascontiguousarray(y_table.T))
     out.append(np.concatenate([high, high, low], axis=1))
+    pick = np.zeros((128, 256))
+    signs = np.zeros((4, 24, 256))
+
+    def place(index, b):
+        return index if b == 0 else (index + 16 if index < 8 else index + 4)
+
+    def enter(out_row, n, col, c_out, c_in):
+        if c_out == c_in:
+            signs[n, out_row, col] = 1.0
+        else:
+            signs[2 + n, out_row, col] = 1.0 if c_out else -1.0
+
+    for m in range(16):
+        owner, b = m // 2, m % 2
+        for c in range(2):
+            for p in range(PLANES):
+                pick[m, 24 * owner + place(6 * c + p, b)] = 1.0
+            pick[m, 192 + 8 * owner + 2 * c + b] = 1.0
+            for n in range(2):
+                for c_out in range(2):
+                    for p in range(PLANES):
+                        enter(
+                            place(6 * c_out + p, n), n, 24 * owner + place(6 * c + p, b), c_out, c
+                        )
+                    enter(2 * c_out + n, n, 192 + 8 * owner + 2 * c + b, c_out, c)
+    out.append(pick.astype(jnp.bfloat16))
+    out.append(signs.reshape(96, 256).astype(np.float32))
     return [jnp.asarray(t) for t in out]
 
 
@@ -91,13 +118,13 @@
 
 def kernel(
     shift_hbm, dij_hbm, kind_hbm, psi_hbm, sticks_hbm, z3_hbm, vloc_hbm, dv_hbm, zt3_hbm, xh_hbm, xl_hbm, xth_hbm, xtl_hbm,
-    yh_hbm, yl_hbm, yt3_hbm, beta_hbm,
+    yh_hbm, yl_hbm, yt3_hbm, pick_hbm, signs_hbm, beta_hbm,
     first_out, second_out, weights_out, cells_out,
-    shift, dij, kind, psi, sticks, z3, vloc_flat, dv_flat, zt3, xh, xl, xth, xtl, yh, yl, yt3,
+    shift, dij, kind, psi, sticks, z3, vloc_flat, dv_flat, zt3, xh, xl, xth, xtl, yh, yl, yt3, pick, signs,
     beta, vloc, dv, cells, occupied, onehot, mask, send, recv, small_send, small_recv,
     part_send, part_recv, lhs, grid, ex, eh, el, dh, dl, psi_field, field0, field1,
-    q, proj, coef, couple, vec, image, kin, own, dens,
-    load_sem, psi_sem, ssem, rsem, rall, tssem, trsem, part_sem,
+    q, found_all, zall, zbh, zbl, psi_proj, proj, coef, couple, vec, image, kin, own, dens,
+    load_sem, psi_sem, z_sem, pp_sem, ssem, rsem, rall, tssem, trsem, part_sem,
 ):
     me = lax.axis_index("ga")
     mb = lax.axis_index("band")
@@ -128,7 +155,7 @@
         kind=(kind_hbm, kind), dij=(dij_hbm, dij), shift=(shift_hbm, shift),
         dv=(dv_hbm, dv_flat), xh=(xh_hbm, xh), xl=(xl_hbm, xl), yh=(yh_hbm, yh),
         yl=(yl_hbm, yl), yt3=(yt3_hbm, yt3), xth=(xth_hbm, xth), xtl=(xtl_hbm, xtl),
-        zt3=(zt3_hbm, zt3), vloc=(vloc_hbm, vloc_flat),
+        zt3=(zt3_hbm, zt3), pick=(pick_hbm, pick), signs=(signs_hbm, signs), vloc=(vloc_hbm, vloc_flat),
         beta=(beta_hbm, beta),
     )
     for at, (name, (source, target)) in enumerate(pairs.items()):
@@ -188,15 +215,47 @@
             small_all(rnd).wait_recv()
         return jnp.sum(small_recv[rnd], axis=0)
 
-    def psi_copy(k):
-        where = (me, lax.rem(mb + k, nb))
-        return copy(psi, occupied.at[mb], psi_sem.at[0], psi_sem.at[1], where)
+    mz, mc = mb // 2, lax.rem(mb, 2)
+    partner = mz * 2 + 1 - mc
+
+    def alike(dz):
+        return lax.rem(mz + dz, 4) * 2 + mc
+
+    def gather_out(block, slot, sems):
+        for dz in (2, 1, 3):
+            copy(block, slot, sems.at[0], sems.at[1], (me, alike(dz))).start()
+        copy(block, slot, sems.at[0], sems.at[2], (me, partner)).start()
+
+    def planes_out(first):
+        some = pl.ds(first, 8)
+        gather_out(recv.at[0, some], zall.at[mb, some], z_sem)
+
+    def gather_bytes(count, held, sems, which):
+        some = held.at[pl.ds(0, count)]
+        return copy(some, some, sems.at[0], sems.at[which], (me, partner))
+
+    def gather_on(held, sems):
+        gather_bytes(3, held, sems, 1).wait_recv()
+        for dz in (1, 3, 2):
+            slot = held.at[alike(dz)]
+            copy(slot, slot, sems.at[0], sems.at[2], (me, partner)).start()
+
+    def gather_done(held, sems):
+        gather_bytes(4, held, sems, 2).wait_recv()
+
+    def gather_sent(held, sems):
+        gather_bytes(7, held, sems, 1).wait_send()
 
     rest = pl.ds(0, nb - 1)
     after = (me, lax.rem(mb + 1, nb))
 
-    def psi_all():
-        return copy(occupied.at[rest], occupied.at[rest], psi_sem.at[0], psi_sem.at[1], after)
+    def proj_copy(k):
+        where = (me, lax.rem(mb + k, nb))
+        return copy(psi_proj.at[16], psi_proj.at[8 + mb], pp_sem.at[0], pp_sem.at[1], where)
+
+    def proj_all():
+        some = psi_proj.at[rest]
+        return copy(some, some, pp_sem.at[0], pp_sem.at[1], after)
 
     def part_copy(k):
         other = lax.rem(mb + k, nb)
@@ -313,18 +372,21 @@
         loads[name].wait()
     with jax.named_scope("couple"):
         couple_all()
+    with jax.named_scope("unpack"):
+        loads["dv"].wait()
+        unpack(dv_flat, dv)
+    zbh[192:256, :] = jnp.zeros((64, 2048), bf16)
+    zbl[192:256, :] = jnp.zeros((64, 2048), bf16)
+    psi_proj[0:8] = jnp.zeros((8, 8, 128), f32)
+    psi_proj[16] = jnp.zeros((8, 128), f32)
+    vec[0] = wide.astype(f32)
     with jax.named_scope("barrier"):
         pl.semaphore_wait(barrier, GROUPS - 1 + nb - 1)
     exchange(0)
 
-    for k in BANDS_FAR:
-        psi_copy(k).start()
+    gather_out(psi, occupied.at[mb], psi_sem)
     occupied[mb] = psi[...]
-
-    with jax.named_scope("unpack"):
-        loads["dv"].wait()
-        unpack(dv_flat, dv)
-    for name in ("xh", "xl", "yh", "yl", "yt3", "xth", "xtl", "zt3"):
+    for name in ("xh", "xl", "yh", "yl", "yt3", "xth", "xtl", "zt3", "pick", "signs"):
         loads[name].wait()
     ones = jnp.ones((256, 128), bf16)
 
@@ -356,7 +418,9 @@
         with jax.named_scope("fill_lhs"):
             if rnd == 0:
                 lax.fori_loop(0, GROUPS, body, 0)
-            else:
+                planes_out(0)
+                zall[mb] = recv[0]
+            elif rnd != 2:
                 arrived(rnd)
         if rnd:
             for src in range(GROUPS):
@@ -391,7 +455,7 @@
                     jnp.concatenate([dh[:, lanes], dl[:, lanes], dh[:, lanes]], axis=0),
                 )
 
-    def to_sticks(rnd, potential, source):
+    def to_sticks(rnd, potential, source, between=None):
         with jax.named_scope("stick_y"):
             for p in range(PLANES):
                 lanes = slice(256 * p, 256 * p + 256)
@@ -428,26 +492,32 @@
                     q[8 * r : 8 * r + 16, lanes] = uh
                     q[192 + 8 * r : 208 + 8 * r, lanes] = ul
 
+        if between is not None:
+            between()
         with jax.named_scope("stick_pick"):
-            for k, dx in enumerate(X_ORDER + (None,)):
-                if dx is not None:
-                    quad = lax.rem(mx + dx, 4)
+            for k in range(6):
+                if k > 1:
+                    dx = X_ORDER[k - 2]
+                    for dy in (2, 1, 3, 0):
+                        if dx or dy:
+                            ga_copy(rnd, peer(dx, dy)).start()
+                if k < 4:
+                    quad = lax.rem(mx + X_ORDER[k], 4)
                     lanes = pl.ds(pl.multiple_of(quad * 512, 512), 512)
-                    both = dot(q[...], onehot[:, lanes])
-                    found = both[0:192] + both[192:384]
-                    picked = jnp.sum(found.reshape(ROWS, 8, 512) * mask[:, lanes][None], axis=1)
+                    found_all[k % 2] = dot(q[...], onehot[:, lanes])
+                if 0 < k < 5:
+                    quad = lax.rem(mx + X_ORDER[k - 1], 4)
+                    lanes = pl.ds(pl.multiple_of(quad * 512, 512), 512)
+                    both = found_all[(k - 1) % 2, 0:192] + found_all[(k - 1) % 2, 192:384]
+                    picked = jnp.sum(both.reshape(ROWS, 8, 512) * mask[:, lanes][None], axis=1)
                     for n in range(4):
                         send[rnd, 4 * quad + n] = picked[:, 128 * n : 128 * n + 128]
-                if k > 0:
-                    for dy in (2, 1, 3, 0):
-                        if X_ORDER[k - 1] or dy:
-                            ga_copy(rnd, peer(X_ORDER[k - 1], dy)).start()
             recv[rnd, me] = send[rnd, me]
 
     def z_forward(rnd):
         return deep(zt3[...], collected(rnd))
 
-    def project(load, count, source):
+    def project(load, count, source, begin=0):
         step = 4
 
         def body(g, c):
@@ -473,7 +543,7 @@
             return c
 
         with jax.named_scope("project"):
-            lax.fori_loop(0, count // step, body, 0)
+            lax.fori_loop(begin // step, count // step, body, 0)
 
     def projections(o, count):
         ph, pl_ = split(proj[o, 0:count, :])
@@ -527,27 +597,80 @@
             occupied[owner, 1, b, at : at + rows, :].astype(f32),
         )
 
+    with jax.named_scope("unpack"):
+        loads["vloc"].wait()
+        unpack(vloc_flat, vloc)
+    loads["beta"].wait()
+    project(beta_rows, 16, vec.at[0])
     fill_planes(0, psi_field)
+    with jax.named_scope("pass_psi"):
+        gather_on(occupied, psi_sem)
     to_sticks(1, dv, psi_field)
-
+    planes_out(8)
+    project(beta_rows, 128, vec.at[0], 16)
+    for o in range(4):
+        psi_proj[16, o : o + 1, :] = projections(o, 128)
+    for k in BANDS_FAR:
+        proj_copy(k).start()
+    psi_proj[8 + mb] = psi_proj[16]
     arrived(1)
     vec[1] = z_forward(1)
-    psi_all().wait_recv()
+    gather_done(occupied, psi_sem)
 
     project(psi_rows, 16, vec.at[1])
     small_send[0] = jnp.zeros((8, 128), f32)
     for o in range(4):
         small_send[0, o : o + 1, 0:16] = projections(o, 16)
     small_exchange(0)
-    with jax.named_scope("unpack"):
-        loads["vloc"].wait()
-        unpack(vloc_flat, vloc)
+    project(beta_rows, 64, vec.at[1])
+    with jax.named_scope("pass_z"):
+        gather_on(zall, z_sem)
+    project(beta_rows, 128, vec.at[1], 64)
+    image_proj = [projections(o, 128) for o in range(4)]
+    proj_all().wait_recv()
+    with jax.named_scope("z_wait"):
+        gather_done(zall, z_sem)
+
+    def halve(src, c):
+        lanes = pl.ds(pl.multiple_of(src * 128, 128), 128)
+        for e in range(4):
+            both = jnp.concatenate([zall[2 * e, src], zall[2 * e + 1, src]], axis=0)
+            uh, ul = split(both)
+            zbh[48 * e : 48 * e + 48, lanes] = uh
+            zbl[48 * e : 48 * e + 48, lanes] = ul
+        return c
+
+    with jax.named_scope("halve"):
+        lax.fori_loop(0, GROUPS, halve, 0)
     found = small_total(0) * (1.0 / (2.0 * GRID * 2048))
-    eye = (row[0:16] == lane[0:16]).astype(f32)
-    spread(eye, found)
-    vec[1] = -vec[1]
-    apply(psi_rows, 16, vec.at[1])
-    vec[0] = image[...]
+    with jax.named_scope("enter"):
+        fh, fl = split(found)
+        laid_out = dot(
+            jnp.concatenate([fh, fl], axis=1), jnp.concatenate([pick[...], pick[...]], axis=0)
+        )
+        entry = jnp.zeros((24, 256), f32)
+        for o in range(4):
+            entry = entry + signs[24 * o : 24 * o + 24, :] * laid_out[o : o + 1, :]
+        nh, nl = split(entry[0:8, 128:256])
+        ph, plow = split(psi_proj[0:16].reshape(128, 128))
+        joined = dot(
+            jnp.concatenate([nh, nl, nh], axis=1), jnp.concatenate([ph, ph, plow], axis=0)
+        )
+        small_send[1] = jnp.zeros((8, 128), f32)
+        for o in range(4):
+            small_send[1, o : o + 1, :] = joined[o : o + 1, :] - image_proj[o]
+        small_exchange(1)
+        mh, ml = split(entry)
+        weights = jnp.concatenate([mh, ml, mh], axis=1)
+        for part in range(4):
+            lanes = slice(512 * part, 512 * part + 512)
+            planes = dot(
+                weights,
+                jnp.concatenate([zbh[:, lanes], zbh[:, lanes], zbl[:, lanes]], axis=0),
+            )
+            for n in range(4):
+                src = 4 * part + n
+                recv[2, src] = planes[:, 128 * n : 128 * n + 128] - send[1, src]
 
     def transform_out(rnd, source):
         dealt(rnd, deep(z3[...], source[...]))
@@ -600,33 +723,36 @@
         )
 
     direction = vec.at[0]
-    transform_out(2, direction)
-    loads["beta"].wait()
-    project(beta_rows, 128, direction)
-    small_send[1] = jnp.zeros((8, 128), f32)
-    for o in range(4):
-        small_send[1, o : o + 1, :] = projections(o, 128)
-    small_send[1, 4:5, :] = packed(stick_sum(direction, direction))
-    small_exchange(1)
-    curves = stick_sum(direction, direction, True)
     fill_planes(2, field0)
     local = grid_sum(field0, field0)
-    small_send[3] = jnp.zeros((8, 128), f32)
-    small_send[3, 0:1, :] = packed([curves[b] + local[b] for b in range(2)])
-    small_exchange(3)
-    to_sticks(3, vloc, field0)
+
+    def rhs():
+        with jax.named_scope("rhs"):
+            eye = (row[0:16] == lane[0:16]).astype(f32)
+            spread(eye, found)
+            vec[1] = -vec[1]
+            apply(psi_rows, 16, vec.at[1])
+            vec[0] = image[...]
+            curves = stick_sum(direction, direction, True)
+            small_send[3] = jnp.zeros((8, 128), f32)
+            small_send[3, 0:1, :] = packed([curves[b] + local[b] for b in range(2)])
+            small_send[3, 1:2, :] = packed(stick_sum(direction, direction))
+            small_exchange(3)
+
+    to_sticks(3, vloc, field0, rhs)
     sums = small_total(1)
     values0 = sums[0:4]
     coupled0 = coupled_rows(sums)[0:4]
     nonlocal0 = band_dots(values0, coupled0)
-    norm0 = unpacked(sums[4:5])
     spread(couple[...], values0)
     for c in range(2):
         for b in range(2):
             at, of = slice(96 * c, 96 * c + 96), slice(128 * b, 128 * b + 128)
             vec[1, at, of] = direction[at, of] * (kin[...] + shift[b])
     apply(beta_rows, 128, vec.at[1])
-    curve0 = [c + n for c, n in zip(unpacked(small_total(3)[0:1]), nonlocal0)]
+    sums = small_total(3)
+    norm0 = unpacked(sums[1:2])
+    curve0 = [c + n for c, n in zip(unpacked(sums[0:1]), nonlocal0)]
     alpha0 = [norm0[b] / curve0[b] for b in range(2)]
     arrived(3)
     image[...] += z_forward(3)
@@ -699,9 +825,12 @@
     weights_out[4:8, :] = jnp.zeros((4, 128), f32)
 
     for rnd in range(5):
-        ga_all(rnd).wait_send()
+        if rnd != 2:
+            ga_all(rnd).wait_send()
         small_all(rnd).wait_send()
-    psi_all().wait_send()
+    gather_sent(occupied, psi_sem)
+    gather_sent(zall, z_sem)
+    proj_all().wait_send()
     with jax.named_scope("part_wait"):
         part_all().wait_recv()
     cells_out[...] = jnp.sum(part_recv[...], axis=0)
@@ -733,7 +862,7 @@
     pieces = pl.pallas_call(
         kernel,
         out_shape=OUTS,
-        in_specs=[pl.BlockSpec(memory_space=pl.ANY)] * 17,
+        in_specs=[pl.BlockSpec(memory_space=pl.ANY)] * 19,
         out_specs=(vmem,) * 4,
         scratch_shapes=[
             pltpu.SMEM((2,), f32),
@@ -769,6 +898,11 @@
             pltpu.VMEM((192, 1536), f32),
             pltpu.VMEM((192, 1536), f32),
             pltpu.VMEM((384, 512), bf16),
+            pltpu.VMEM((2, 384, 512), f32),
+            pltpu.VMEM((8, GROUPS, ROWS, 128), f32),
+            pltpu.VMEM((256, 2048), bf16),
+            pltpu.VMEM((256, 2048), bf16),
+            pltpu.VMEM((17, 8, 128), f32),
             pltpu.VMEM((4, 128, 128), f32),
             pltpu.VMEM((4, 128, 128), f32),
             pltpu.VMEM((128, 128), f32),
@@ -777,7 +911,9 @@
             pltpu.VMEM((GRID, 128), f32),
             pltpu.VMEM((8, 2048), f32),
             pltpu.VMEM((192, 1536), f32),
-            dma((17,)),
+            dma((19,)),
+            dma((3,)),
+            dma((3,)),
             dma((2,)),
             dma((5,)),
             dma((GROUPS,)),

time: 63.2 us -> 59.4 us (0.940)
  Pallas kernels: 62.4 us -> 58.7 us
    pallas_call x1, Pallas kernels: 61.7 us -> 57.9 us  [per_device(): pl.pallas_call(kernel, out_shape=OUTS, in_specs=[pl.BlockSpec(memory_spac...]
where the time goes in v5:
time: 59.4 us; the launch traced here: 59.3 us
  Pallas kernels  58.7 us (99%)
  between operations  0.64 us (1%)
    pallas_call x1, Pallas kernels, per_device(): pl.pallas_call(kernel, out_shape=OUTS, in_specs=[pl.BlockSpec(memory_spac...  57.9 us

profile of v5, /device:TPU:1, one launch (start us, length us, event | category | flops | bytes accessed | tf_op | source)
XLA Modules:
  0.0 59.3 jit_solution(983429774760252909)
XLA Ops:
  0.6 57.9 %shard_map.194 = (f32[192,256]{1,0:T(8,128)S(1)}, f32[192,256]{1,0:T(8,128)S(1)}, f32[8,128]{1,0:T(8,128)S(1)}, f32[72,128]{1,0:T(8,128)S(1)}) custom-call(f32[2]{0:T(128)} %shift_hbm.1, f32[2,4,4]{2,1,0:T(4,128)} %dij_hbm.1, s32[32]{0:T(128)} %kind_hbm.1, bf16[2,2,96,128]{3,2,1,0:T(8,128)(2,1)} %psi_hbm.1, s32[16,128]{1,0:T(8,128)} %bitcast.1, ...), custom_call_target="tpu_custom_call" | custom-call | tf_op jit(solution)/shard_map/pallas_call | solution.py:862
  58.6 0.7 %shard_map.195 = (f32[2,2,96,128]{3,2,1,0:T(8,128)}, f32[6,1152]{1,0:T(8,128)}) custom-call(f32[192,256]{1,0:T(8,128)S(1)} %get-tuple-element.6.first, f32[192,256]{1,0:T(8,128)S(1)} %get-tuple-element.7.second, f32[8,128]{1,0:T(8,128)S(1)} %get-tuple-element.8.weights, f32[72,128]{1,0:T(8,128)S(1)} %get-tuple-element.9.cells), custom_call_target="tpu_custom_call" | custom-call | tf_op jit(solution)/shard_map/pallas_call | solution.py:932

commit v6 on v5

--- a/solution.py
+++ b/solution.py
@@ -226,10 +226,6 @@
             copy(block, slot, sems.at[0], sems.at[1], (me, alike(dz))).start()
         copy(block, slot, sems.at[0], sems.at[2], (me, partner)).start()
 
-    def planes_out(first):
-        some = pl.ds(first, 8)
-        gather_out(recv.at[0, some], zall.at[mb, some], z_sem)
-
     def gather_bytes(count, held, sems, which):
         some = held.at[pl.ds(0, count)]
         return copy(some, some, sems.at[0], sems.at[which], (me, partner))
@@ -418,7 +414,7 @@
         with jax.named_scope("fill_lhs"):
             if rnd == 0:
                 lax.fori_loop(0, GROUPS, body, 0)
-                planes_out(0)
+                gather_out(recv.at[0], zall.at[mb], z_sem)
                 zall[mb] = recv[0]
             elif rnd != 2:
                 arrived(rnd)
@@ -518,7 +514,7 @@
         return deep(zt3[...], collected(rnd))
 
     def project(load, count, source, begin=0):
-        step = 4
+        step = 8
 
         def body(g, c):
             sums = [[None] * 4 for _ in range(step)]
@@ -603,11 +599,11 @@
     loads["beta"].wait()
     project(beta_rows, 16, vec.at[0])
     fill_planes(0, psi_field)
+    to_sticks(1, dv, psi_field)
+    project(beta_rows, 80, vec.at[0], 16)
     with jax.named_scope("pass_psi"):
         gather_on(occupied, psi_sem)
-    to_sticks(1, dv, psi_field)
-    planes_out(8)
-    project(beta_rows, 128, vec.at[0], 16)
+    project(beta_rows, 128, vec.at[0], 80)
     for o in range(4):
         psi_proj[16, o : o + 1, :] = projections(o, 128)
     for k in BANDS_FAR:
@@ -641,7 +637,7 @@
         return c
 
     with jax.named_scope("halve"):
-        lax.fori_loop(0, GROUPS, halve, 0)
+        lax.fori_loop(0, GROUPS, halve, 0, unroll=4)
     found = small_total(0) * (1.0 / (2.0 * GRID * 2048))
     with jax.named_scope("enter"):
         fh, fl = split(found)

time: 59.4 us -> 58.8 us (0.990)
  Pallas kernels: 58.7 us -> 58 us
    pallas_call x1, Pallas kernels: 57.9 us -> 57.3 us  [per_device(): pl.pallas_call(kernel, out_shape=OUTS, in_specs=[pl.BlockSpec(memory_spac...]
where the time goes in v6:
time: 58.8 us; the launch traced here: 58.7 us
  Pallas kernels  58 us (99%)
  between operations  0.64 us (1%)
    pallas_call x1, Pallas kernels, per_device(): pl.pallas_call(kernel, out_shape=OUTS, in_specs=[pl.BlockSpec(memory_spac...  57.3 us

profile of v6, /device:TPU:1, one launch (start us, length us, event | category | flops | bytes accessed | tf_op | source)
XLA Modules:
  0.0 58.7 jit_solution(5059027794982096052)
XLA Ops:
  0.6 57.3 %shard_map.194 = (f32[192,256]{1,0:T(8,128)S(1)}, f32[192,256]{1,0:T(8,128)S(1)}, f32[8,128]{1,0:T(8,128)S(1)}, f32[72,128]{1,0:T(8,128)S(1)}) custom-call(f32[2]{0:T(128)} %shift_hbm.1, f32[2,4,4]{2,1,0:T(4,128)} %dij_hbm.1, s32[32]{0:T(128)} %kind_hbm.1, bf16[2,2,96,128]{3,2,1,0:T(8,128)(2,1)} %psi_hbm.1, s32[16,128]{1,0:T(8,128)} %bitcast.1, ...), custom_call_target="tpu_custom_call" | custom-call | tf_op jit(solution)/shard_map/pallas_call | solution.py:858
  57.9 0.7 %shard_map.195 = (f32[2,2,96,128]{3,2,1,0:T(8,128)}, f32[6,1152]{1,0:T(8,128)}) custom-call(f32[192,256]{1,0:T(8,128)S(1)} %get-tuple-element.6.first, f32[192,256]{1,0:T(8,128)S(1)} %get-tuple-element.7.second, f32[8,128]{1,0:T(8,128)S(1)} %get-tuple-element.8.weights, f32[72,128]{1,0:T(8,128)S(1)} %get-tuple-element.9.cells), custom_call_target="tpu_custom_call" | custom-call | tf_op jit(solution)/shard_map/pallas_call | solution.py:928

commit v7 on v6

--- a/solution.py
+++ b/solution.py
@@ -559,8 +559,8 @@
         for z in range(GRID // rows):
 
             def body(g, acc):
-                for t in range(4):
-                    j = g * 4 + t
+                for t in range(8):
+                    j = g * 8 + t
                     p0, p1 = load(j, z * rows, rows)
                     out = []
                     for b in range(2):
@@ -577,7 +577,7 @@
                 for c in range(2)
             )
             with jax.named_scope("apply"):
-                done = lax.fori_loop(0, count // 4, body, init)
+                done = lax.fori_loop(0, count // 8, body, init)
             for b in range(2):
                 for c in range(2):
                     at = 96 * c + z * rows

time: 58.8 us -> 58.7 us (level)
  no operation moved by 1% of the time
where the time goes in v7:
time: 58.7 us; the launch traced here: 58.6 us
  Pallas kernels  57.9 us (99%)
  between operations  0.64 us (1%)
    pallas_call x1, Pallas kernels, per_device(): pl.pallas_call(kernel, out_shape=OUTS, in_specs=[pl.BlockSpec(memory_spac...  57.2 us

profile of v7, /device:TPU:1, one launch (start us, length us, event | category | flops | bytes accessed | tf_op | source)
XLA Modules:
  0.0 58.6 jit_solution(9343188102344141925)
XLA Ops:
  0.6 57.2 %shard_map.194 = (f32[192,256]{1,0:T(8,128)S(1)}, f32[192,256]{1,0:T(8,128)S(1)}, f32[8,128]{1,0:T(8,128)S(1)}, f32[72,128]{1,0:T(8,128)S(1)}) custom-call(f32[2]{0:T(128)} %shift_hbm.1, f32[2,4,4]{2,1,0:T(4,128)} %dij_hbm.1, s32[32]{0:T(128)} %kind_hbm.1, bf16[2,2,96,128]{3,2,1,0:T(8,128)(2,1)} %psi_hbm.1, s32[16,128]{1,0:T(8,128)} %bitcast.1, ...), custom_call_target="tpu_custom_call" | custom-call | tf_op jit(solution)/shard_map/pallas_call | solution.py:858
  57.8 0.7 %shard_map.195 = (f32[2,2,96,128]{3,2,1,0:T(8,128)}, f32[6,1152]{1,0:T(8,128)}) custom-call(f32[192,256]{1,0:T(8,128)S(1)} %get-tuple-element.6.first, f32[192,256]{1,0:T(8,128)S(1)} %get-tuple-element.7.second, f32[8,128]{1,0:T(8,128)S(1)} %get-tuple-element.8.weights, f32[72,128]{1,0:T(8,128)S(1)} %get-tuple-element.9.cells), custom_call_target="tpu_custom_call" | custom-call | tf_op jit(solution)/shard_map/pallas_call | solution.py:928
